TPU v7x, 32 devices: a whole 2x2x4 slice. The times are simulated.
32 devices in a mesh: dom: 4 (over z), col: 8 (over y, x, core).
Axes of the slice: x: 2, y: 2, z: 4, core: 2. Of those that a mesh axis runs over, the one named last changes fastest.
Arguments:
- rhs_interior: bfloat16 [4, 48, 8192], P('dom', 'col'), may hold values from -6 to 6
- interior_inv: bfloat16 [4, 8192, 8192], P('dom', None, 'col'), may hold values from -0.0625 to 0.0625
- coupling: bfloat16 [4, 8192, 768], P('dom', 'col'), may hold values from -0.0625 to 0.0625
- rhs_interface: bfloat16 [48, 8192], P('col', 'dom'), may hold values from -6 to 6
- block_ids: int32 [4, 6], P('dom'), may hold values from 0 to 63, as said below
- interface_inv: bfloat16 [8192, 8192], P('dom', 'col'), may hold values from -0.0625 to 0.0625
Outputs:
- interior_solution: bfloat16 [4, 48, 8192], P('dom', None, 'col')
- interface_solution: bfloat16 [48, 8192], P('col')
Inputs may be any that keep to these rules, and one draw needn't show every extreme that they name: `block_ids`: each row names 6 different blocks.
All inputs are finite; a program needn't handle non-finite values.
Results may differ from a plain program's by a relative error of at most 0.025.
Values may be sent and summed in bfloat16 or wider, within the bound.
No kernel may reach another device: no remote copies, remote signals or barrier semaphores. Data moves between devices by JAX's collectives and lax.ppermute only.
A program may use at most 64 MiB of HBM per device.

v0:
```python
import jax
import jax.numpy as jnp
from jax import lax
from jax.sharding import PartitionSpec as P

G = 8192
BS = 128


def per_device(rhs_interior, interior_inv, coupling, rhs_interface, block_ids, interface_inv):
    rhs_local = rhs_interior[0]
    inverse = interior_inv[0]
    couple = coupling[0]
    blocks = block_ids[0]
    row_count = rhs_local.shape[0]
    block_count = blocks.shape[0]
    nblocks = G // BS
    onehot = (blocks[:, None] == jnp.arange(nblocks, dtype=jnp.int32)[None, :]).astype(jnp.float32)
    interior_step = jnp.dot(
        lax.all_gather(rhs_local, "col", axis=0, tiled=True),
        inverse,
        preferred_element_type=jnp.float32,
    ).astype(jnp.bfloat16)
    contribution = lax.psum_scatter(
        jnp.dot(interior_step, couple, preferred_element_type=jnp.float32).astype(jnp.bfloat16),
        "col",
        scatter_dimension=0,
        tiled=True,
    ).astype(jnp.float32)
    placed = jnp.einsum(
        "kb,rks->rbs", onehot, contribution.reshape(row_count, block_count, BS)
    ).reshape(row_count, G)
    summed = lax.psum_scatter(
        placed.astype(jnp.bfloat16), "dom", scatter_dimension=1, tiled=True
    ).astype(jnp.float32)
    reduced = (rhs_interface.astype(jnp.float32) - summed).astype(jnp.bfloat16)
    partial_solution = jnp.dot(
        lax.all_gather(reduced, "col", axis=0, tiled=True),
        interface_inv,
        preferred_element_type=jnp.float32,
    )
    column_total = lax.psum(partial_solution.astype(jnp.bfloat16), "dom")
    solution = lax.all_to_all(column_total, "col", split_axis=0, concat_axis=1, tiled=True)
    local_solution = jnp.einsum(
        "kb,rbs->rks",
        onehot.astype(jnp.bfloat16),
        solution.reshape(row_count, nblocks, BS),
        preferred_element_type=jnp.float32,
    )
    local_solution = local_solution.reshape(row_count, block_count * BS).astype(jnp.bfloat16)
    every_solution = lax.all_gather(local_solution, "col", axis=0, tiled=True)
    correction = jnp.einsum("rl,il->ri", every_solution, couple, preferred_element_type=jnp.float32)
    rhs_columns = lax.all_to_all(rhs_local, "col", split_axis=1, concat_axis=0, tiled=True)
    interior_rhs = (rhs_columns.astype(jnp.float32) - correction).astype(jnp.bfloat16)
    result = jnp.dot(
        lax.all_gather(interior_rhs, "col", axis=1, tiled=True),
        inverse,
        preferred_element_type=jnp.float32,
    )
    interior_solution = result.astype(jnp.bfloat16)[None]
    return (interior_solution, solution)


def solution(mesh):
    placed = (
        P("dom", "col", None),
        P("dom", None, "col"),
        P("dom", "col", None),
        P("col", "dom"),
        P("dom", None),
        P("dom", "col"),
    )
    return jax.shard_map(
        per_device,
        mesh=mesh,
        in_specs=placed,
        out_specs=(P("dom", None, "col"), P("col", None)),
        check_vma=False,
    )
```

profile of v0, /device:TPU:0, one launch (start us, length us, event | category | flops | bytes accessed | tf_op | source)
XLA Modules:
  0.0 168.0 jit_solution(9237124908893844768)
XLA Ops:
  7.2 0.0 reduce-scatter.4.cloned.1.call-start
  7.2 1.2 copy.15
  8.4 14.6 %all-gather = bf16[1,48,8192]{2,0,1:T(2,128)(2,1)S(1)} all-gather(bf16[1,6,8192]{2,0,1:T(2,128)(2,1)S(1)} %copy.15), channel_id=2, replica_groups=mesh['dom'=4,'col'=8] {'col'}, dimensions={1}, use_global_device_ids=true | all-gather | bytes 884736 | tf_op jit(solution)/shard_map/all_gather | solution.py:20
  23.0 9.5 %fusion.21 = bf16[48,768]{1,0:T(8,128)(2,1)S(1)} fusion(bf16[1,1024,768]{2,1,0:T(8,128)(2,1)S(1)} %copy-done, bf16[1,8192,1024]{2,1,0:T(8,128)(2,1)} %param.7, bf16[1,48,8192]{2,0,1:T(2,128)(2,1)S(1)} %all-gather), kind=kOutput, calls=%fused_computation.14 | convolution fusion | flops 880889856 | bytes 19210240 | tf_op jit(solution)/shard_map/dot_general | solution.py:25
  32.6 14.5 %fusion = bf16[8,768]{1,0:T(8,128)(2,1)S(1)} fusion(bf16[48,768]{1,0:T(8,128)(2,1)S(1)} %fusion.21), kind=kCustom, calls=%all-reduce-scatter | all-reduce-scatter fusion | flops 49153 | bytes 86528
  47.1 1.3 collective-permute-start
  48.4 2.0 %collective-permute-start.1 = (bf16[6,768]{1,0:T(8,128)(2,1)S(1)}, bf16[6,768]{1,0:T(8,128)(2,1)S(1)}, u32[]{:S(2)}, u32[]{:S(2)}) collective-permute-start(bf16[6,768]{1,0:T(8,128)(2,1)S(1)} %slice), channel_id=1, source_target_pairs={{0,2},{1,3},{2,4},{3,5},{4,6},{5,7},{8,10},{9,11},{10,12},{11,13},... | collective-permute-start | bytes 27656
  50.4 0.6 dynamic-slice.4
  51.7 0.1 collective-permute-done.1
  51.8 0.2 concatenate
  52.1 0.3 fusion.24
  52.4 0.7 copy.25
  53.1 0.0 reduce-scatter.4.cloned.1.call-update
  53.1 0.0 all-reduce.4.cloned.1.call-start
  53.2 23.2 %reduce-scatter.4.cloned.1.call-done = bf16[6,2048]{1,0:T(8,128)(2,1)} async-done(((bf16[6,8192]{1,0:T(8,128)(2,1)}), bf16[6,2048]{1,0:T(8,128)(2,1)}) %reduce-scatter.4.cloned.1.call-update) | async-done | bytes 24592 | tf_op jit(solution)/shard_map/reduce_scatter | solution.py:33
  76.4 0.8 fusion.35
  77.1 9.3 %all-gather.1 = bf16[8,6,2048]{2,1,0:T(8,128)(2,1)S(1)} all-gather(bf16[1,6,2048]{2,1,0:T(8,128)(2,1)S(1)} %fusion.35), channel_id=1, replica_groups=mesh['dom'=4,'col'=8] {'col'}, dimensions={0}, use_global_device_ids=true | all-gather | bytes 221184 | tf_op jit(solution)/shard_map/all_gather | solution.py:38
  86.4 0.1 reshape.30
  86.5 3.0 %convolution_convert_fusion = bf16[48,1024]{1,0:T(8,128)(2,1)S(1)} fusion(bf16[48,2048]{1,0:T(8,128)(2,1)S(1)} %reshape.30, bf16[2048,1024]{1,0:T(8,128)(2,1)} %param.11), kind=kOutput, calls=%fused_computation.12 | convolution fusion | flops 201375744 | bytes 4489216 | tf_op jit(solution)/shard_map/dot_general | solution.py:37
  89.5 0.7 all_to_all.26
  90.2 0.0 all-reduce.4.cloned.1.call-update
  90.2 8.0 %all_to_all.32 = bf16[6,8,1024]{2,0,1:T(8,128)(2,1)S(1)} all-to-all(bf16[6,8,1024]{2,0,1:T(8,128)(2,1)S(1)} %bitcast.65), channel_id=1, replica_groups=mesh['dom'=4,'col'=8] {'col'}, dimensions={1} | all-to-all | bytes 196608 | tf_op jit(solution)/shard_map/all_to_all | solution.py:53
  98.3 24.0 %all-reduce.4.cloned.1.call-done = bf16[8,6,1024]{2,1,0:T(8,128)(2,1)} async-done(((bf16[8,6,1024]{2,1,0:T(8,128)(2,1)}), bf16[8,6,1024]{2,1,0:T(8,128)(2,1)}) %all-reduce.4.cloned.1.call-update) | async-done | bytes 98320 | tf_op jit(solution)/shard_map/psum | solution.py:42
  122.3 3.6 %all-to-all-start.1 = ((bf16[8,6,1024]{2,1,0:T(8,128)(2,1)}), bf16[8,6,1024]{2,1,0:T(8,128)(2,1)S(1)}, u32[]{:S(2)}, u32[]{:S(2)}) async-start(bf16[8,6,1024]{2,1,0:T(8,128)(2,1)} %all-reduce.4.cloned.1.call-done), calls=%async_computation.2 | async-start | bytes 262144 | tf_op jit(solution)/shard_map/all_to_all | solution.py:43
  126.0 5.4 %all-to-all-done.1 = bf16[8,6,1024]{2,1,0:T(8,128)(2,1)S(1)} async-done(((bf16[8,6,1024]{2,1,0:T(8,128)(2,1)}), bf16[8,6,1024]{2,1,0:T(8,128)(2,1)S(1)}, u32[]{:S(2)}, u32[]{:S(2)}) %all-to-all-start.1) | async-done | bytes 98336 | tf_op jit(solution)/shard_map/all_to_all | solution.py:43
  131.4 0.1 copy.16
  131.5 0.2 fusion.28
  131.7 8.3 %all-gather.2 = bf16[8,6,768]{2,1,0:T(8,128)(2,1)S(1)} all-gather(bf16[1,6,768]{2,1,0:T(8,128)(2,1)S(1)} %reshape.31), channel_id=1, replica_groups=mesh['dom'=4,'col'=8] {'col'}, dimensions={0}, use_global_device_ids=true | all-gather | bytes 82944 | tf_op jit(solution)/shard_map/all_gather | solution.py:51
  140.1 0.6 fusion.12
  140.6 10.4 %all_gather.15 = bf16[48,8192]{1,0:T(8,128)(2,1)S(1)} all-gather(bf16[48,1024]{1,0:T(8,128)(2,1)S(1)} %fusion.12), channel_id=1, replica_groups=mesh['dom'=4,'col'=8] {'col'}, dimensions={1}, use_global_device_ids=true | all-gather | bytes 884736 | tf_op jit(solution)/shard_map/all_gather | solution.py:56
  151.0 9.5 %fusion.25 = bf16[1,48,1024]{2,1,0:T(8,128)(2,1)} fusion(bf16[48,8192]{1,0:T(8,128)(2,1)S(1)} %all_gather.15, bf16[1,8192,1024]{2,1,0:T(8,128)(2,1)} %param.7), kind=kOutput, calls=%fused_computation.16 | convolution fusion | flops 805355520 | bytes 17661952 | tf_op jit(solution)/shard_map/dot_general | solution.py:55
  160.5 0.7 copy.28
  (19 shorter events, 0.2 us)
Async XLA Ops:
  7.2 15.9 %copy-start = (bf16[1,1024,768]{2,1,0:T(8,128)(2,1)S(1)}, bf16[1,1024,768]{2,1,0:T(8,128)(2,1)}, u32[]{:S(2)}) copy-start(bf16[1,1024,768]{2,1,0:T(8,128)(2,1)} %param.8) | copy-start | bytes 4718596
  7.2 69.2 %reduce-scatter.4.cloned.1.call-start = ((), (), s32[]{:S(2)}) async-start(), calls=%async_computation.3 | async-start | bytes 163840 | tf_op jit(solution)/shard_map/reduce_scatter | solution.py:33
  23.0 27.4 %copy-start.3 = (u32[32]{0:T(128)S(1)}, u32[32]{0:T(128)}, u32[]{:S(2)}) copy-start(u32[32]{0:T(128)} %constant.7) | copy-start | bytes 388
  23.0 29.0 %copy-start.4 = (s32[1,6]{1,0:T(1,128)S(1)}, s32[1,6]{1,0:T(1,128)}, u32[]{:S(2)}) copy-start(s32[1,6]{1,0:T(1,128)} %param.10) | copy-start | bytes 76
  23.0 53.3 %copy-start.2 = (bf16[6,2048]{1,0:T(8,128)(2,1)S(1)}, bf16[6,2048]{1,0:T(8,128)(2,1)}, u32[]{:S(2)}) copy-start(bf16[6,2048]{1,0:T(8,128)(2,1)} %param.9) | copy-start | bytes 73732
  32.6 57.6 %copy-start.1 = (bf16[1,6,8192]{2,1,0:T(8,128)(2,1)S(1)}, bf16[1,6,8192]{2,1,0:T(8,128)(2,1)}, u32[]{:S(2)}) copy-start(bf16[1,6,8192]{2,1,0:T(8,128)(2,1)} %param.6) | copy-start | bytes 294916
  47.1 4.7 %collective-permute-start = (bf16[8,768]{1,0:T(8,128)(2,1)S(1)}, bf16[8,768]{1,0:T(8,128)(2,1)S(1)}, u32[]{:S(2)}, u32[]{:S(2)}) collective-permute-start(bf16[8,768]{1,0:T(8,128)(2,1)S(1)} %fusion), channel_id=1, source_target_pairs={{0,1},{1,2},{2,3},{3,4},{4,5},{5,6},{6,7},{8,9},{9,10},{10,11},{11... | collective-permute-start | bytes 36872
  48.4 3.4 %collective-permute-start.1 = (bf16[6,768]{1,0:T(8,128)(2,1)S(1)}, bf16[6,768]{1,0:T(8,128)(2,1)S(1)}, u32[]{:S(2)}, u32[]{:S(2)}) collective-permute-start(bf16[6,768]{1,0:T(8,128)(2,1)S(1)} %slice), channel_id=1, source_target_pairs={{0,2},{1,3},{2,4},{3,5},{4,6},{5,7},{8,10},{9,11},{10,12},{11,13},... | collective-permute-start | bytes 27656
  53.1 69.1 %all-reduce.4.cloned.1.call-start = ((), (), s32[]{:S(2)}) async-start(), calls=%async_computation.4 | async-start | bytes 262144 | tf_op jit(solution)/shard_map/psum | solution.py:42
  122.3 9.1 %all-to-all-start.1 = ((bf16[8,6,1024]{2,1,0:T(8,128)(2,1)}), bf16[8,6,1024]{2,1,0:T(8,128)(2,1)S(1)}, u32[]{:S(2)}, u32[]{:S(2)}) async-start(bf16[8,6,1024]{2,1,0:T(8,128)(2,1)} %all-reduce.4.cloned.1.call-done), calls=%async_computation.2 | async-start | bytes 262144 | tf_op jit(solution)/shard_map/all_to_all | solution.py:43
Sparse Core Ops, SparseCore 0:
  53.3 23.0 reduce-scatter.3
  90.3 31.8 all-reduce.3
where the time goes:
time: 169 us; the launch traced here: 168 us
  blocking collectives  65 us (38%)
  waiting for transfers between devices  52.8 us (31%)
  matrix products  23.1 us (14%)
  between operations  14.9 us (9%)
  starting transfers between devices  7.03 us (4%)
  local copies, waits for them, and re-layouts  4.39 us (3%)
    psum x1, waiting for transfers between devices, per_device(): column_total = lax.psum(partial_solution.astype(jnp.bfloat16), 'dom')  24 us
    reduce_scatter x1, waiting for transfers between devices, per_device(): lax.psum_scatter(placed.astype(jnp.bfloat16), 'dom', scatter_dimension=1,...  23.2 us
    all_gather x1, blocking collectives, per_device(): lax.all_gather(rhs_local, 'col', axis=0, tiled=True)  14.6 us
    unnamed x1, blocking collectives  14.5 us
    all_gather x1, blocking collectives, per_device(): lax.all_gather(interior_rhs, 'col', axis=1, tiled=True)  10.4 us
    dot_general x1, matrix products, per_device(): jnp.dot(interior_step, couple, preferred_element_type=jnp.float32)  9.54 us
    dot_general x1, matrix products, per_device(): jnp.dot(lax.all_gather(interior_rhs, 'col', axis=1, tiled=True), inverse,...  9.46 us
    all_gather x1, blocking collectives, per_device(): lax.all_gather(reduced, 'col', axis=0, tiled=True)  9.25 us
  transfers between devices with their start and end apart: 5, of which 4 were waited for; matrix products, arithmetic and copies ran while one was open for 0% of the time, Pallas kernels for 0%

commit v1 on v0

v1 whole, which is shorter than its diff:
```python
import jax
import jax.numpy as jnp
from jax import lax
from jax.sharding import PartitionSpec as P


def exchange(value, axis):
    size = lax.axis_size(axis)
    pieces = [value]
    for shift in range(1, size):
        pairs = [(source, (source + shift) % size) for source in range(size)]
        pieces.append(lax.ppermute(value, axis, pairs))
    return pieces


def per_device(rhs_interior, interior_inv, coupling, rhs_interface, block_ids, interface_inv):
    rhs_local = rhs_interior[0]
    inverse = interior_inv[0]
    couple = coupling[0]
    blocks = block_ids[0]
    row_count, interior_count = rhs_local.shape
    block_count = blocks.shape[0]
    block_size = couple.shape[1] // block_count
    col_size = lax.axis_size("col")
    dom_size = lax.axis_size("dom")
    rows = row_count * col_size
    slice_width = rhs_interface.shape[1]
    slice_blocks = slice_width // block_size
    nblocks = slice_blocks * dom_size
    own_columns = couple.shape[0]
    col = lax.axis_index("col")
    dom = lax.axis_index("dom")

    every_blocks = jnp.stack(exchange(blocks, "dom"))
    joined = jnp.concatenate([rhs_local, rhs_interface], axis=1)
    gathered = lax.all_gather(joined, "col", axis=0, tiled=True)
    rhs_all = gathered[:, :interior_count]
    interface_rows = gathered[:, interior_count:]

    step = jnp.dot(rhs_all, inverse, preferred_element_type=jnp.float32).astype(jnp.bfloat16)
    partial = jnp.dot(step, couple, preferred_element_type=jnp.float32).astype(jnp.bfloat16)
    partials = lax.all_gather(partial, "col", axis=0)
    contribution = jnp.sum(partials.astype(jnp.float32), axis=0).astype(jnp.bfloat16)
    contributions = jnp.stack(exchange(contribution, "dom"))
    local_ids = every_blocks - dom * slice_blocks
    onehot = (local_ids[:, :, None] == jnp.arange(slice_blocks, dtype=jnp.int32)).astype(jnp.bfloat16)
    summed = jnp.einsum(
        "dkb,drks->rbs",
        onehot,
        contributions.reshape(dom_size, rows, block_count, block_size),
        preferred_element_type=jnp.float32,
    ).reshape(rows, slice_width)
    reduced = (interface_rows.astype(jnp.float32) - summed).astype(jnp.bfloat16)
    part_solution = jnp.dot(
        reduced, interface_inv, preferred_element_type=jnp.float32
    ).astype(jnp.bfloat16)
    total = sum(piece.astype(jnp.float32) for piece in exchange(part_solution, "dom"))
    every_total = lax.all_gather(total.astype(jnp.bfloat16), "col", axis=1, tiled=True)
    solution = lax.dynamic_slice_in_dim(every_total, col * row_count, row_count, axis=0)
    picks = (blocks[:, None] == jnp.arange(nblocks, dtype=jnp.int32)).astype(jnp.bfloat16)
    local_solution = jnp.einsum(
        "kb,rbs->rks",
        picks,
        every_total.reshape(rows, nblocks, block_size),
        preferred_element_type=jnp.float32,
    ).reshape(rows, block_count * block_size).astype(jnp.bfloat16)
    correction = jnp.einsum("rl,il->ri", local_solution, couple, preferred_element_type=jnp.float32)
    rhs_columns = lax.dynamic_slice_in_dim(rhs_all, col * own_columns, own_columns, axis=1)
    interior_rhs = (rhs_columns.astype(jnp.float32) - correction).astype(jnp.bfloat16)
    result = jnp.dot(
        lax.all_gather(interior_rhs, "col", axis=1, tiled=True),
        inverse,
        preferred_element_type=jnp.float32,
    )
    return (result.astype(jnp.bfloat16)[None], solution)


def solution(mesh):
    placed = (
        P("dom", "col", None),
        P("dom", None, "col"),
        P("dom", "col", None),
        P("col", "dom"),
        P("dom", None),
        P("dom", "col"),
    )
    return jax.shard_map(
        per_device,
        mesh=mesh,
        in_specs=placed,
        out_specs=(P("dom", None, "col"), P("col", None)),
        check_vma=False,
    )
```

time: 169 us -> 98.6 us (0.58)
  waiting for transfers between devices: 52.8 us -> 14.1 us
  blocking collectives: 65 us -> 42.3 us
  between operations: 14.9 us -> 0.79 us
  starting transfers between devices: 7.03 us -> 13.3 us
    psum x1 -> x0, waiting for transfers between devices: 24 us -> none  [per_device(): column_total = lax.psum(partial_solution.astype(jnp.bfloat16), 'dom')]
    reduce_scatter x1 -> x0, waiting for transfers between devices: 23.2 us -> none  [per_device(): lax.psum_scatter(placed.astype(jnp.bfloat16), 'dom', scatter_dimension=1,...]
    unnamed x1 -> x0, blocking collectives: 14.5 us -> none
    ppermute x0 -> x9, waiting for transfers between devices: none -> 14.1 us  [exchange(): pieces.append(lax.ppermute(value, axis, pairs))]
    ppermute x0 -> x9, starting transfers between devices: none -> 13.3 us  [exchange(): pieces.append(lax.ppermute(value, axis, pairs))]
    all_to_all x1 -> x0, blocking collectives: 8.04 us -> none  [per_device(): lax.all_to_all(rhs_local, 'col', split_axis=1, concat_axis=0, tiled=True)]
    all_to_all x1 -> x0, waiting for transfers between devices: 5.44 us -> none  [per_device(): lax.all_to_all(column_total, 'col', split_axis=0, concat_axis=1, tiled=True)]
    all_to_all x1 -> x0, starting transfers between devices: 3.64 us -> none  [per_device(): lax.all_to_all(column_total, 'col', split_axis=0, concat_axis=1, tiled=True)]
  transfers between devices with their start and end apart: 5 -> 9, of which waited for: 4 -> 4; matrix products, arithmetic and copies ran while one was open for 0% -> 12% of each run, Pallas kernels for 0% -> 0%
where the time goes in v1:
time: 98.6 us; the launch traced here: 98.3 us
  blocking collectives  42.3 us (43%)
  matrix products  22.9 us (23%)
  waiting for transfers between devices  14.1 us (14%)
  starting transfers between devices  13.3 us (13%)
  local copies, waits for them, and re-layouts  2.85 us (3%)
  other arithmetic  2.05 us (2%)
    ppermute x9, waiting for transfers between devices, exchange(): pieces.append(lax.ppermute(value, axis, pairs))  14.1 us
    ppermute x9, starting transfers between devices, exchange(): pieces.append(lax.ppermute(value, axis, pairs))  13.3 us
    all_gather x1, blocking collectives, per_device(): gathered = lax.all_gather(joined, 'col', axis=0, tiled=True)  12.9 us
    all_gather x1, blocking collectives, per_device(): lax.all_gather(interior_rhs, 'col', axis=1, tiled=True)  9.91 us
    all_gather x1, blocking collectives, per_device(): lax.all_gather(total.astype(jnp.bfloat16), 'col', axis=1, tiled=True)  9.89 us
    all_gather x1, blocking collectives, per_device(): partials = lax.all_gather(partial, 'col', axis=0)  9.5 us
    dot_general x1, matrix products, per_device(): jnp.dot(lax.all_gather(interior_rhs, 'col', axis=1, tiled=True), inverse,...  9.46 us
    dot_general x1, matrix products, per_device(): jnp.dot(step, couple, preferred_element_type=jnp.float32)  9.12 us
  transfers between devices with their start and end apart: 9, of which 4 were waited for; matrix products, arithmetic and copies ran while one was open for 12% of the time, Pallas kernels for 0%

profile of v1, /device:TPU:0, one launch (start us, length us, event | category | flops | bytes accessed | tf_op | source)
XLA Modules:
  0.0 98.3 jit_solution(5120586478832418925)
XLA Ops:
  0.6 5.1 %collective-permute-start.5 = (s32[6]{0:T(128)}, s32[6]{0:T(128)S(1)}, u32[]{:S(2)}, u32[]{:S(2)}) collective-permute-start(s32[6]{0:T(128)} %bitcast.74), channel_id=1, source_target_pairs={{0,24},{8,0},{16,8},{24,16},{1,25},{9,1},{17,9},{25,17},{2,26},{10... | collective-permute-start | bytes 80 | tf_op jit(solution)/shard_map/ppermute | solution.py:12
  5.8 1.0 %collective-permute-start.3 = (s32[6]{0:T(128)}, s32[6]{0:T(128)S(1)}, u32[]{:S(2)}, u32[]{:S(2)}) collective-permute-start(s32[6]{0:T(128)} %bitcast.76), channel_id=1, source_target_pairs={{0,8},{8,16},{16,24},{24,0},{1,9},{9,17},{17,25},{25,1},{2,10},{10... | collective-permute-start | bytes 80 | tf_op jit(solution)/shard_map/ppermute | solution.py:12
  6.8 1.0 maximum_bitcast_fusion
  7.7 12.9 %all-gather.1 = bf16[8,6,10240]{2,1,0:T(8,128)(2,1)} all-gather(bf16[1,6,10240]{2,1,0:T(8,128)(2,1)S(1)} %maximum_bitcast_fusion), channel_id=1, replica_groups=mesh['dom'=4,'col'=8] {'col'}, dimensions={0}, use_global_device_ids=true | all-gather | bytes 1105920 | tf_op jit(solution)/shard_map/all_gather | solution.py:36
  20.7 1.5 %reshape.58 = bf16[48,10240]{1,0:T(8,128)(2,1)S(1)} reshape(bf16[8,6,10240]{2,1,0:T(8,128)(2,1)} %all-gather.1) | data formatting | bytes 1966080
  22.2 9.1 %fusion.20 = bf16[48,768]{1,0:T(8,128)(2,1)S(1)} fusion(bf16[1,1024,768]{2,1,0:T(8,128)(2,1)S(1)} %copy-done, bf16[1,8192,1024]{2,1,0:T(8,128)(2,1)} %param.7, bf16[48,10240]{1,0:T(8,128)(2,1)S(1)} %reshape.58), kind=kOutput, calls=%fused_computation.14 | convolution fusion | flops 880889856 | bytes 19210240 | tf_op jit(solution)/shard_map/dot_general | solution.py:41
  31.3 9.5 %all-gather = bf16[384,768]{1,0:T(8,128)(2,1)S(1)} all-gather(bf16[48,768]{1,0:T(8,128)(2,1)S(1)} %fusion.20), channel_id=2, replica_groups=mesh['dom'=4,'col'=8] {'col'}, dimensions={0}, use_global_device_ids=true | all-gather | bytes 663552 | tf_op jit(solution)/shard_map/all_gather | solution.py:42
  40.8 0.1 reduce_sum.12
  40.9 2.9 %collective-permute-start.2 = (bf16[48,768]{1,0:T(8,128)(2,1)S(1)}, bf16[48,768]{1,0:T(8,128)(2,1)S(1)}, u32[]{:S(2)}, u32[]{:S(2)}) collective-permute-start(bf16[48,768]{1,0:T(8,128)(2,1)S(1)} %reduce_sum.12), channel_id=1, source_target_pairs={{0,24},{8,0},{16,8},{24,16},{1,25},{9,1},{17,9},{25,17},{2,26},{10... | collective-permute-start | bytes 221192 | tf_op jit(solution)/shard_map/ppermute | solution.py:12
  43.8 1.1 %collective-permute-start.1 = (bf16[48,768]{1,0:T(8,128)(2,1)S(1)}, bf16[48,768]{1,0:T(8,128)(2,1)S(1)}, u32[]{:S(2)}, u32[]{:S(2)}) collective-permute-start(bf16[48,768]{1,0:T(8,128)(2,1)S(1)} %reduce_sum.12), channel_id=1, source_target_pairs={{0,16},{8,24},{16,0},{24,8},{1,17},{9,25},{17,1},{25,9},{2,18},{10... | collective-permute-start | bytes 221192 | tf_op jit(solution)/shard_map/ppermute | solution.py:12
  44.9 0.1 stack.27
  45.0 0.1 collective-permute-start
  45.1 1.3 %collective-permute-done.2 = bf16[48,768]{1,0:T(8,128)(2,1)S(1)} collective-permute-done((bf16[48,768]{1,0:T(8,128)(2,1)S(1)}, bf16[48,768]{1,0:T(8,128)(2,1)S(1)}, u32[]{:S(2)}, u32[]{:S(2)}) %collective-permute-start.2) | collective-permute-done | bytes 73760 | tf_op jit(solution)/shard_map/ppermute | solution.py:12
  46.5 0.1 stack.30
  46.6 5.6 %collective-permute-done.1 = bf16[48,768]{1,0:T(8,128)(2,1)S(1)} collective-permute-done((bf16[48,768]{1,0:T(8,128)(2,1)S(1)}, bf16[48,768]{1,0:T(8,128)(2,1)S(1)}, u32[]{:S(2)}, u32[]{:S(2)}) %collective-permute-start.1) | collective-permute-done | bytes 73760 | tf_op jit(solution)/shard_map/ppermute | solution.py:12
  52.2 0.1 stack.29
  52.3 0.1 stack.28
  52.4 0.4 fusion.29
  52.8 3.0 %convolution_convert_fusion = bf16[48,1024]{1,0:T(8,128)(2,1)S(1)} fusion(bf16[2048,1024]{1,0:T(8,128)(2,1)} %param.11, f32[6,8,16,128]{3,2,1,0:T(8,128)S(1)} %bitcast.67, bf16[48,10240]{1,0:T(8,128)(2,1)S(1)} %reshape.58), kind=kOutput, calls=%fused_computation.12 | convolution fusion | flops 201670656 | bytes 4882432 | tf_op jit(solution)/shard_map/dot_general | solution.py:54
  55.8 1.3 %collective-permute-start.8 = (bf16[48,1024]{1,0:T(8,128)(2,1)S(1)}, bf16[48,1024]{1,0:T(8,128)(2,1)S(1)}, u32[]{:S(2)}, u32[]{:S(2)}) collective-permute-start(bf16[48,1024]{1,0:T(8,128)(2,1)S(1)} %convolution_convert_fusion), channel_id=1, source_target_pairs={{0,24},{8,0},{16,8},{24,16},{1,25},{9,1},{17,9},{25,17},{2,26},{10... | collective-permute-start | bytes 294920 | tf_op jit(solution)/shard_map/ppermute | solution.py:12
  57.1 1.9 %collective-permute-start.6 = (bf16[48,1024]{1,0:T(8,128)(2,1)S(1)}, bf16[48,1024]{1,0:T(8,128)(2,1)}, u32[]{:S(2)}, u32[]{:S(2)}) collective-permute-start(bf16[48,1024]{1,0:T(8,128)(2,1)S(1)} %convolution_convert_fusion), channel_id=1, source_target_pairs={{0,8},{8,16},{16,24},{24,0},{1,9},{9,17},{17,25},{25,1},{2,10},{10... | collective-permute-start | bytes 294920 | tf_op jit(solution)/shard_map/ppermute | solution.py:12
  58.9 0.1 slice.8
  59.0 2.3 %collective-permute-done.8 = bf16[48,1024]{1,0:T(8,128)(2,1)S(1)} collective-permute-done((bf16[48,1024]{1,0:T(8,128)(2,1)S(1)}, bf16[48,1024]{1,0:T(8,128)(2,1)S(1)}, u32[]{:S(2)}, u32[]{:S(2)}) %collective-permute-start.8) | collective-permute-done | bytes 98336 | tf_op jit(solution)/shard_map/ppermute | solution.py:12
  61.4 4.9 %collective-permute-done.7 = bf16[48,1024]{1,0:T(8,128)(2,1)} collective-permute-done((bf16[48,1024]{1,0:T(8,128)(2,1)S(1)}, bf16[48,1024]{1,0:T(8,128)(2,1)}, u32[]{:S(2)}, u32[]{:S(2)}) %collective-permute-start.7) | collective-permute-done | bytes 98336 | tf_op jit(solution)/shard_map/ppermute | solution.py:12
  66.2 1.0 %add_convert_fusion = bf16[48,1024]{1,0:T(8,128)(2,1)S(1)} fusion(bf16[48,1024]{1,0:T(8,128)(2,1)S(1)} %collective-permute-done.8, bf16[48,1024]{1,0:T(8,128)(2,1)} %collective-permute-done.7, bf16[48,1024]{1,0:T(8,128)(2,1)} %collective-permute-done.6, bf16[48,1024]{1,0:T(8,128)(2,1)S(1)} %convolution_convert_fusion), kind=kLoop, calls=%fused_computation.27 | loop fusion | flops 393216 | bytes 491520 | tf_op jit(solution)/shard_map/convert_element_type | solution.py:58
  67.2 9.9 %all_gather.18 = bf16[48,8192]{1,0:T(8,128)(2,1)S(1)} all-gather(bf16[48,1024]{1,0:T(8,128)(2,1)S(1)} %add_convert_fusion), channel_id=1, replica_groups=mesh['dom'=4,'col'=8] {'col'}, dimensions={1}, use_global_device_ids=true | all-gather | bytes 884736 | tf_op jit(solution)/shard_map/all_gather | solution.py:58
  77.1 0.7 constant_dynamic-slice_fusion
  77.8 0.2 copy.18
  78.0 0.3 convolution_convert_fusion.1
  78.3 0.6 fusion.11
  78.9 9.9 %all_gather.19 = bf16[48,8192]{1,0:T(8,128)(2,1)S(1)} all-gather(bf16[48,1024]{1,0:T(8,128)(2,1)S(1)} %fusion.11), channel_id=1, replica_groups=mesh['dom'=4,'col'=8] {'col'}, dimensions={1}, use_global_device_ids=true | all-gather | bytes 884736 | tf_op jit(solution)/shard_map/all_gather | solution.py:71
  88.8 9.5 %fusion.23 = bf16[1,48,1024]{2,1,0:T(8,128)(2,1)} fusion(bf16[48,8192]{1,0:T(8,128)(2,1)S(1)} %all_gather.19, bf16[1,8192,1024]{2,1,0:T(8,128)(2,1)} %param.7), kind=kOutput, calls=%fused_computation.15 | convolution fusion | flops 805355520 | bytes 17661952 | tf_op jit(solution)/shard_map/dot_general | solution.py:70
  (12 shorter events, 0.0 us)
Async XLA Ops:
  0.6 21.6 %copy-start = (bf16[1,1024,768]{2,1,0:T(8,128)(2,1)S(1)}, bf16[1,1024,768]{2,1,0:T(8,128)(2,1)}, u32[]{:S(2)}) copy-start(bf16[1,1024,768]{2,1,0:T(8,128)(2,1)} %param.8) | copy-start | bytes 4718596
  0.6 44.4 %collective-permute-start.5 = (s32[6]{0:T(128)}, s32[6]{0:T(128)S(1)}, u32[]{:S(2)}, u32[]{:S(2)}) collective-permute-start(s32[6]{0:T(128)} %bitcast.74), channel_id=1, source_target_pairs={{0,24},{8,0},{16,8},{24,16},{1,25},{9,1},{17,9},{25,17},{2,26},{10... | collective-permute-start | bytes 80 | tf_op jit(solution)/shard_map/ppermute | solution.py:12
  5.8 39.3 %collective-permute-start.4 = (s32[6]{0:T(128)}, s32[6]{0:T(128)S(1)}, u32[]{:S(2)}, u32[]{:S(2)}) collective-permute-start(s32[6]{0:T(128)} %bitcast.75), channel_id=1, source_target_pairs={{0,16},{8,24},{16,0},{24,8},{1,17},{9,25},{17,1},{25,9},{2,18},{10... | collective-permute-start | bytes 80 | tf_op jit(solution)/shard_map/ppermute | solution.py:12
  5.8 39.3 %collective-permute-start.3 = (s32[6]{0:T(128)}, s32[6]{0:T(128)S(1)}, u32[]{:S(2)}, u32[]{:S(2)}) collective-permute-start(s32[6]{0:T(128)} %bitcast.76), channel_id=1, source_target_pairs={{0,8},{8,16},{16,24},{24,0},{1,9},{9,17},{17,25},{25,1},{2,10},{10... | collective-permute-start | bytes 80 | tf_op jit(solution)/shard_map/ppermute | solution.py:12
  22.2 22.9 %copy-start.1 = (s32[1,6]{1,0:T(1,128)S(1)}, s32[1,6]{1,0:T(1,128)}, u32[]{:S(2)}) copy-start(s32[1,6]{1,0:T(1,128)} %param.10) | copy-start | bytes 76
  40.9 5.6 %collective-permute-start.2 = (bf16[48,768]{1,0:T(8,128)(2,1)S(1)}, bf16[48,768]{1,0:T(8,128)(2,1)S(1)}, u32[]{:S(2)}, u32[]{:S(2)}) collective-permute-start(bf16[48,768]{1,0:T(8,128)(2,1)S(1)} %reduce_sum.12), channel_id=1, source_target_pairs={{0,24},{8,0},{16,8},{24,16},{1,25},{9,1},{17,9},{25,17},{2,26},{10... | collective-permute-start | bytes 221192 | tf_op jit(solution)/shard_map/ppermute | solution.py:12
  43.8 8.4 %collective-permute-start.1 = (bf16[48,768]{1,0:T(8,128)(2,1)S(1)}, bf16[48,768]{1,0:T(8,128)(2,1)S(1)}, u32[]{:S(2)}, u32[]{:S(2)}) collective-permute-start(bf16[48,768]{1,0:T(8,128)(2,1)S(1)} %reduce_sum.12), channel_id=1, source_target_pairs={{0,16},{8,24},{16,0},{24,8},{1,17},{9,25},{17,1},{25,9},{2,18},{10... | collective-permute-start | bytes 221192 | tf_op jit(solution)/shard_map/ppermute | solution.py:12
  45.0 7.2 %collective-permute-start = (bf16[48,768]{1,0:T(8,128)(2,1)S(1)}, bf16[48,768]{1,0:T(8,128)(2,1)S(1)}, u32[]{:S(2)}, u32[]{:S(2)}) collective-permute-start(bf16[48,768]{1,0:T(8,128)(2,1)S(1)} %reduce_sum.12), channel_id=1, source_target_pairs={{0,8},{8,16},{16,24},{24,0},{1,9},{9,17},{17,25},{25,1},{2,10},{10... | collective-permute-start | bytes 221192 | tf_op jit(solution)/shard_map/ppermute | solution.py:12
  55.8 5.6 %collective-permute-start.8 = (bf16[48,1024]{1,0:T(8,128)(2,1)S(1)}, bf16[48,1024]{1,0:T(8,128)(2,1)S(1)}, u32[]{:S(2)}, u32[]{:S(2)}) collective-permute-start(bf16[48,1024]{1,0:T(8,128)(2,1)S(1)} %convolution_convert_fusion), channel_id=1, source_target_pairs={{0,24},{8,0},{16,8},{24,16},{1,25},{9,1},{17,9},{25,17},{2,26},{10... | collective-permute-start | bytes 294920 | tf_op jit(solution)/shard_map/ppermute | solution.py:12
  57.1 9.2 %collective-permute-start.7 = (bf16[48,1024]{1,0:T(8,128)(2,1)S(1)}, bf16[48,1024]{1,0:T(8,128)(2,1)}, u32[]{:S(2)}, u32[]{:S(2)}) collective-permute-start(bf16[48,1024]{1,0:T(8,128)(2,1)S(1)} %convolution_convert_fusion), channel_id=1, source_target_pairs={{0,16},{8,24},{16,0},{24,8},{1,17},{9,25},{17,1},{25,9},{2,18},{10... | collective-permute-start | bytes 294920 | tf_op jit(solution)/shard_map/ppermute | solution.py:12
  57.1 9.2 %collective-permute-start.6 = (bf16[48,1024]{1,0:T(8,128)(2,1)S(1)}, bf16[48,1024]{1,0:T(8,128)(2,1)}, u32[]{:S(2)}, u32[]{:S(2)}) collective-permute-start(bf16[48,1024]{1,0:T(8,128)(2,1)S(1)} %convolution_convert_fusion), channel_id=1, source_target_pairs={{0,8},{8,16},{16,24},{24,0},{1,9},{9,17},{17,25},{25,1},{2,10},{10... | collective-permute-start | bytes 294920 | tf_op jit(solution)/shard_map/ppermute | solution.py:12

commit v2 on v0

v2 whole, which is shorter than its diff:
```python
import functools

import jax
import jax.numpy as jnp
from jax import lax
from jax.experimental import pallas as pl
from jax.experimental.pallas import tpu as pltpu
from jax.sharding import PartitionSpec as P

LANES = 128
CORES = 2
BF16 = jnp.bfloat16
F32 = jnp.float32
WHOLE = pl.BlockSpec(memory_space=pltpu.VMEM)


def run(kernel, outputs, operands, flops, scratch=(), limit=8):
    return pl.pallas_call(
        kernel,
        out_shape=[jax.ShapeDtypeStruct(shape, BF16) for shape in outputs],
        in_specs=[WHOLE] * len(operands),
        out_specs=[WHOLE] * len(outputs),
        scratch_shapes=list(scratch),
        compiler_params=pltpu.CompilerParams(vmem_limit_bytes=limit * 2**20),
        cost_estimate=pl.CostEstimate(flops=flops, bytes_accessed=2**20, transcendentals=0),
    )(*[pltpu.with_memory_space_constraint(operand, pltpu.VMEM) for operand in operands])


def pairs_of(size, shift, stride=1):
    members = size // stride
    xor = members & (members - 1) == 0
    pairs = []
    for source in range(size):
        unit, rest = divmod(source, stride)
        target = unit ^ shift if xor else (unit + shift) % members
        pairs.append((source, target * stride + rest))
    return pairs


def exchange(value, axis, stride=1):
    size = lax.axis_size(axis)
    return [
        lax.ppermute(value, axis, pairs_of(size, shift, stride))
        for shift in range(1, size // stride)
    ]


def dot(left, right):
    return jnp.dot(left, right, preferred_element_type=F32)


def forward_kernel(half_rows, gathered, inverse, couple, keep, give, rhs):
    slabs, row_count, _ = gathered.shape
    interior = inverse.shape[0]
    order = [slab for core in range(CORES) for slab in range(core, slabs, CORES)]
    for place, slab in enumerate(order):
        rhs[place * row_count : (place + 1) * row_count, :] = gathered[slab, :, :interior]
    step = dot(rhs[...], inverse[...]).astype(BF16)
    part = dot(step, couple[...]).astype(BF16)
    core = lax.rem(lax.axis_index("col"), CORES)

    @pl.when(core == 0)
    def _():
        keep[...] = part[:half_rows]
        give[...] = part[half_rows:]

    @pl.when(core == 1)
    def _():
        keep[...] = part[half_rows:]
        give[...] = part[:half_rows]


def join_kernel(local, interface, out, sems):
    interior = local.shape[1]
    first = pltpu.make_async_copy(local, out.at[:, :interior], sems.at[0])
    second = pltpu.make_async_copy(interface, out.at[:, interior:], sems.at[1])
    first.start()
    second.start()
    first.wait()
    second.wait()


def add_kernel(*refs):
    out = refs[-1]
    total = refs[0][...].astype(F32)
    for ref in refs[1:-1]:
        total = total + ref[...].astype(F32)
    out[...] = total.astype(BF16)


def pack_kernel(block_count, *refs):
    ids, out = refs[-2], refs[-1]
    width = refs[0].shape[1]
    total = refs[0][...].astype(F32)
    for ref in refs[1:-2]:
        total = total + ref[...].astype(F32)
    out[:, :width] = total.astype(BF16)
    out[:, width:] = jnp.broadcast_to(ids[...].astype(F32), (out.shape[0], LANES)).astype(BF16)


def place_kernel(block_count, block_size, gathered, *refs):
    pieces, out = refs[:-1], refs[-1]
    row_count = gathered.shape[1]
    rows, width = out.shape
    interior = gathered.shape[2] - width
    core = lax.rem(lax.axis_index("col"), CORES)
    base = (lax.axis_index("dom") * (width // block_size)).astype(F32)
    span = block_count * block_size
    ids = []
    for piece in pieces:
        tail = piece[:, span:].astype(F32) - base
        for block in range(block_count):
            ids.append(jnp.broadcast_to(tail[:, block : block + 1], (rows, block_size)))
    for target in range(width // block_size):
        lanes = slice(target * block_size, (target + 1) * block_size)
        total = jnp.zeros((rows, block_size), F32)
        for index, name in enumerate(ids):
            piece, block = divmod(index, block_count)
            held = pieces[piece][:, block * block_size : (block + 1) * block_size]
            total = total + jnp.where(name == float(target), held.astype(F32), 0.0)
        source = slice(interior + lanes.start, interior + lanes.stop)
        for chip in range(rows // row_count):
            part = slice(chip * row_count, (chip + 1) * row_count)
            have = gathered[CORES * chip + core, :, source].astype(F32)
            out[part, lanes] = (have - total[part]).astype(BF16)


def interface_kernel(mine, other, inverse, out, reduced):
    core = lax.rem(lax.axis_index("col"), CORES)
    rows = mine.shape[0]

    @pl.when(core == 0)
    def _():
        reduced[:rows] = mine[...]
        reduced[rows:] = other[...]

    @pl.when(core == 1)
    def _():
        reduced[:rows] = other[...]
        reduced[rows:] = mine[...]

    out[...] = dot(reduced[...], inverse[...]).astype(BF16)


def backward_kernel(block_size, ids, total, gathered, couple, out, solution, picked):
    slabs, rows, columns = total.shape
    row_count = gathered.shape[1]
    own_columns = couple.shape[0]
    block_count = couple.shape[1] // block_size
    per_slab = columns // block_size
    col = lax.axis_index("col")
    for block in range(block_count):
        name = ids[0, block]
        slab = lax.div(name, per_slab)
        offset = pl.multiple_of(lax.rem(name, per_slab) * block_size, block_size)
        picked[:, block * block_size : (block + 1) * block_size] = total[slab, :, pl.ds(offset, block_size)]
    row = lax.broadcasted_iota(jnp.int32, (rows, rows), 0)
    place = lax.broadcasted_iota(jnp.int32, (rows, rows), 1)
    owner = lax.div(row, row_count)
    held = (
        lax.rem(owner, CORES) * (rows // CORES)
        + lax.div(owner, CORES) * row_count
        + lax.rem(row, row_count)
    )
    turn = (held == place).astype(F32).astype(BF16)
    local = dot(turn, picked[...]).astype(BF16)
    correction = lax.dot_general(
        local, couple[...], (((1,), (1,)), ((), ())), preferred_element_type=F32
    )
    start = pl.multiple_of(col * own_columns, LANES)
    for slab in range(slabs):
        part = slice(slab * row_count, (slab + 1) * row_count)
        have = gathered[slab, :, pl.ds(start, own_columns)].astype(F32)
        out[part] = (have - correction[part]).astype(BF16)
    first = lax.rem(col, CORES) * (rows // CORES) + lax.div(col, CORES) * row_count
    pick_row = lax.broadcasted_iota(jnp.int32, (8, rows), 0)
    pick_place = lax.broadcasted_iota(jnp.int32, (8, rows), 1)
    pick = (pick_row + first == pick_place).astype(F32).astype(BF16)
    for slab in range(slabs):
        chosen = dot(pick, total[slab])[:row_count]
        solution[:, slab * columns : (slab + 1) * columns] = chosen.astype(BF16)


def last_kernel(every, inverse, out, rhs):
    slabs, rows, columns = every.shape
    for slab in range(slabs):
        rhs[:, slab * columns : (slab + 1) * columns] = every[slab]
    out[...] = dot(rhs[...], inverse[...]).astype(BF16)


def per_device(rhs_interior, interior_inv, coupling, rhs_interface, block_ids, interface_inv):
    rhs_local = rhs_interior[0]
    inverse = interior_inv[0]
    couple = coupling[0]
    row_count, interior = rhs_local.shape
    own_columns, local_count = couple.shape
    block_count = block_ids.shape[1]
    block_size = local_count // block_count
    col_size = lax.axis_size("col")
    rows = row_count * col_size
    half = rows // CORES
    width = rhs_interface.shape[1]
    columns = interface_inv.shape[1]

    joined = pl.pallas_call(
        join_kernel,
        out_shape=jax.ShapeDtypeStruct((row_count, interior + width), BF16),
        in_specs=[pl.BlockSpec(memory_space=pltpu.HBM)] * 2,
        out_specs=WHOLE,
        scratch_shapes=[pltpu.SemaphoreType.DMA((2,))],
        compiler_params=pltpu.CompilerParams(vmem_limit_bytes=8 * 2**20),
        cost_estimate=pl.CostEstimate(
            flops=64 * rows * columns * interior, bytes_accessed=2**20, transcendentals=0
        ),
    )(
        pltpu.with_memory_space_constraint(rhs_local, pltpu.HBM),
        pltpu.with_memory_space_constraint(rhs_interface, pltpu.HBM),
    )
    gathered = lax.all_gather(joined, "col", axis=0)
    ids_row = jnp.pad(block_ids, ((0, 0), (0, LANES - block_count)))

    keep, give = run(
        functools.partial(forward_kernel, half),
        [(half, local_count)] * 2,
        [gathered, inverse, couple],
        2 * rows * own_columns * (interior + local_count),
        [pltpu.VMEM((rows, interior), BF16)],
        limit=12,
    )
    other = lax.ppermute(give, "col", [(source, source ^ 1) for source in range(col_size)])
    (pair,) = run(add_kernel, [(half, local_count)], [keep, other], half * local_count)
    (packed,) = run(
        functools.partial(pack_kernel, block_count),
        [(half, local_count + LANES)],
        [pair, *exchange(pair, "col", CORES), ids_row],
        half * local_count,
    )
    (reduced,) = run(
        functools.partial(place_kernel, block_count, block_size),
        [(half, width)],
        [gathered, packed, *exchange(packed, "dom")],
        rows * width * 64,
        limit=16,
    )
    reduced_other = lax.ppermute(reduced, "col", [(source, source ^ 1) for source in range(col_size)])
    (part_solution,) = run(
        interface_kernel,
        [(rows, columns)],
        [reduced, reduced_other, interface_inv],
        2 * rows * width * columns,
        [pltpu.VMEM((rows, width), BF16)],
    )
    (total,) = run(
        add_kernel,
        [(rows, columns)],
        [part_solution, *exchange(part_solution, "dom")],
        rows * columns,
    )
    every_total = lax.all_gather(total, "col", axis=0)
    interior_rhs, solution = pl.pallas_call(
        functools.partial(backward_kernel, block_size),
        out_shape=[
            jax.ShapeDtypeStruct((rows, own_columns), BF16),
            jax.ShapeDtypeStruct((row_count, columns * col_size), BF16),
        ],
        in_specs=[pl.BlockSpec(memory_space=pltpu.SMEM)] + [WHOLE] * 3,
        out_specs=[WHOLE] * 2,
        scratch_shapes=[pltpu.VMEM((rows, local_count), BF16)],
        compiler_params=pltpu.CompilerParams(vmem_limit_bytes=8 * 2**20),
        cost_estimate=pl.CostEstimate(
            flops=2 * rows * own_columns * local_count, bytes_accessed=2**20, transcendentals=0
        ),
    )(
        block_ids,
        pltpu.with_memory_space_constraint(every_total, pltpu.VMEM),
        pltpu.with_memory_space_constraint(gathered, pltpu.VMEM),
        pltpu.with_memory_space_constraint(couple, pltpu.VMEM),
    )
    every_rhs = lax.all_gather(interior_rhs, "col", axis=0)
    (result,) = run(
        last_kernel,
        [(rows, own_columns)],
        [every_rhs, inverse],
        2 * rows * own_columns * interior,
        [pltpu.VMEM((rows, interior), BF16)],
    )
    return (result[None], solution)


def solution(mesh):
    placed = (
        P("dom", "col", None),
        P("dom", None, "col"),
        P("dom", "col", None),
        P("col", "dom"),
        P("dom", None),
        P("dom", "col"),
    )
    return jax.shard_map(
        per_device,
        mesh=mesh,
        in_specs=placed,
        out_specs=(P("dom", None, "col"), P("col", None)),
        check_vma=False,
    )
```

time: 169 us -> 75.5 us (0.45)
  waiting for transfers between devices: 52.8 us -> 16.2 us
  blocking collectives: 65 us -> 33.6 us
  matrix products: 23.1 us -> 0 us
  between operations: 14.9 us -> 0.77 us
  Pallas kernels: 0 us -> 11.7 us
  starting transfers between devices: 7.03 us -> 13 us
  local copies, waits for them, and re-layouts: 4.39 us -> 0.04 us
    psum x1 -> x0, waiting for transfers between devices: 24 us -> none  [per_device(): column_total = lax.psum(partial_solution.astype(jnp.bfloat16), 'dom')]
    reduce_scatter x1 -> x0, waiting for transfers between devices: 23.2 us -> none  [per_device(): lax.psum_scatter(placed.astype(jnp.bfloat16), 'dom', scatter_dimension=1,...]
    dot_general x6 -> x0, matrix products: 23.1 us -> none  [the longest x1 9.54 us: per_device(): jnp.dot(interior_step, couple, preferred_element_type=jnp.float32)]
    ppermute x0 -> x11, waiting for transfers between devices: none -> 16.2 us  [the longest x9 14 us: exchange(): lax.ppermute(value, axis, pairs_of(size, shift, stride))]
    unnamed x1 -> x0, blocking collectives: 14.5 us -> none
    ppermute x0 -> x11, starting transfers between devices: none -> 13 us  [the longest x9 12.5 us: exchange(): lax.ppermute(value, axis, pairs_of(size, shift, stride))]
    pallas_call x0 -> x9, Pallas kernels: none -> 11.7 us  [the longest x7 8.62 us: run(): pl.pallas_call(kernel, out_shape=[jax.ShapeDtypeStruct(shape, BF16) for s...]
    all_gather x4 -> x3, blocking collectives: 42.5 us -> 33.6 us  [the longest x1 13.8 us: per_device(): gathered = lax.all_gather(joined, 'col', axis=0)]
  transfers between devices with their start and end apart: 5 -> 11, of which waited for: 4 -> 9; matrix products, arithmetic and copies ran while one was open for 0% -> 0% of each run, Pallas kernels for 0% -> 0%
where the time goes in v2:
time: 75.5 us; the launch traced here: 75.3 us
  blocking collectives  33.6 us (45%)
  waiting for transfers between devices  16.2 us (21%)
  starting transfers between devices  13 us (17%)
  Pallas kernels  11.7 us (15%)
  between operations  0.77 us (1%)
    ppermute x9, waiting for transfers between devices, exchange(): lax.ppermute(value, axis, pairs_of(size, shift, stride))  14 us
    all_gather x1, blocking collectives, per_device(): gathered = lax.all_gather(joined, 'col', axis=0)  13.8 us
    ppermute x9, starting transfers between devices, exchange(): lax.ppermute(value, axis, pairs_of(size, shift, stride))  12.5 us
    all_gather x1, blocking collectives, per_device(): every_total = lax.all_gather(total, 'col', axis=0)  10 us
    all_gather x1, blocking collectives, per_device(): every_rhs = lax.all_gather(interior_rhs, 'col', axis=0)  9.78 us
    pallas_call x7, Pallas kernels, run(): pl.pallas_call(kernel, out_shape=[jax.ShapeDtypeStruct(shape, BF16) for s...  8.62 us
    pallas_call x1, Pallas kernels, per_device(): pl.pallas_call(functools.partial(backward_kernel, block_size), out_shape=...  1.97 us
  transfers between devices with their start and end apart: 11, of which 9 were waited for; matrix products, arithmetic and copies ran while one was open for 0% of the time, Pallas kernels for 0%

profile of v2, /device:TPU:0, one launch (start us, length us, event | category | flops | bytes accessed | tf_op | source)
XLA Modules:
  0.0 75.3 jit_solution(16281135185482744448)
XLA Ops:
  0.6 0.0 slice-start.1
  0.7 1.1 %shard_map.77 = bf16[6,10240]{1,0:T(8,128)(2,1)S(1)} custom-call(bf16[6,8192]{1,0:T(8,128)(2,1)} %bitcast.17, bf16[6,2048]{1,0:T(8,128)(2,1)} %interface.1), custom_call_target="tpu_custom_call" | custom-call | flops 25769803776 | bytes 1048576 | tf_op jit(solution)/shard_map/pallas_call | solution.py:205
  1.8 13.8 %all-gather.3.gathered = bf16[8,6,10240]{2,1,0:T(8,128)(2,1)S(1)} all-gather(bf16[1,6,10240]{2,1,0:T(8,128)(2,1)S(1)} %bitcast.15), channel_id=2, replica_groups=mesh['dom'=4,'col'=8] {'col'}, dimensions={0}, use_global_device_ids=true | all-gather | bytes 1105920 | tf_op jit(solution)/shard_map/all_gather | solution.py:219
  15.6 0.0 copy-start.2
  15.6 0.0 copy-start.1
  15.7 3.4 %shard_map.78 = (bf16[24,768]{1,0:T(8,128)(2,1)S(1)}, bf16[24,768]{1,0:T(8,128)(2,1)S(1)}) custom-call(bf16[8,6,10240]{2,1,0:T(8,128)(2,1)S(1)} %all-gather.3.gathered, bf16[8192,1024]{1,0:T(8,128)(2,1)S(1)} %bitcast.9, bf16[1024,768]{1,0:T(8,128)(2,1)S(1)} %bitcast.11), custom_call_target="tpu_custom_call" | custom-call | flops 880803840 | bytes 1048576 | tf_op jit(solution)/shard_map/pallas_call | solution.py:18
  19.1 0.5 collective-permute-start
  19.5 0.9 %collective-permute-done.refs_1_ = bf16[24,768]{1,0:T(8,128)(2,1)S(1)} collective-permute-done((bf16[24,768]{1,0:T(8,128)(2,1)S(1)}, bf16[24,768]{1,0:T(8,128)(2,1)S(1)}, u32[]{:S(2)}, u32[]{:S(2)}) %collective-permute-start) | collective-permute-done | bytes 36896 | tf_op jit(solution)/shard_map/ppermute | solution.py:230
  20.4 1.5 %collective-permute-start.3 = (bf16[24,768]{1,0:T(8,128)(2,1)S(1)}, bf16[24,768]{1,0:T(8,128)(2,1)S(1)}, u32[]{:S(2)}, u32[]{:S(2)}) collective-permute-start(bf16[24,768]{1,0:T(8,128)(2,1)S(1)} %shard_map.79.refs_0_), channel_id=1, source_target_pairs={{0,6},{1,7},{2,4},{3,5},{4,2},{5,3},{6,0},{7,1},{8,14},{9,15},{10,... | collective-permute-start | bytes 110600 | tf_op jit(solution)/shard_map/ppermute | solution.py:43
  21.9 0.9 %collective-permute-start.2 = (bf16[24,768]{1,0:T(8,128)(2,1)S(1)}, bf16[24,768]{1,0:T(8,128)(2,1)S(1)}, u32[]{:S(2)}, u32[]{:S(2)}) collective-permute-start(bf16[24,768]{1,0:T(8,128)(2,1)S(1)} %shard_map.79.refs_0_), channel_id=1, source_target_pairs={{0,4},{1,5},{2,6},{3,7},{4,0},{5,1},{6,2},{7,3},{8,12},{9,13},{10,... | collective-permute-start | bytes 110600 | tf_op jit(solution)/shard_map/ppermute | solution.py:43
  22.8 1.1 %collective-permute-start.1 = (bf16[24,768]{1,0:T(8,128)(2,1)S(1)}, bf16[24,768]{1,0:T(8,128)(2,1)S(1)}, u32[]{:S(2)}, u32[]{:S(2)}) collective-permute-start(bf16[24,768]{1,0:T(8,128)(2,1)S(1)} %shard_map.79.refs_0_), channel_id=1, source_target_pairs={{0,2},{1,3},{2,0},{3,1},{4,6},{5,7},{6,4},{7,5},{8,10},{9,11},{10,... | collective-permute-start | bytes 110600 | tf_op jit(solution)/shard_map/ppermute | solution.py:43
  24.0 1.4 %collective-permute-done.3.refs_3_ = bf16[24,768]{1,0:T(8,128)(2,1)S(1)} collective-permute-done((bf16[24,768]{1,0:T(8,128)(2,1)S(1)}, bf16[24,768]{1,0:T(8,128)(2,1)S(1)}, u32[]{:S(2)}, u32[]{:S(2)}) %collective-permute-start.3) | collective-permute-done | bytes 36896 | tf_op jit(solution)/shard_map/ppermute | solution.py:43
  25.3 0.6 collective-permute-done.2.refs_2_
  25.9 0.9 %collective-permute-done.1.refs_1_ = bf16[24,768]{1,0:T(8,128)(2,1)S(1)} collective-permute-done((bf16[24,768]{1,0:T(8,128)(2,1)S(1)}, bf16[24,768]{1,0:T(8,128)(2,1)S(1)}, u32[]{:S(2)}, u32[]{:S(2)}) %collective-permute-start.1) | collective-permute-done | bytes 36896 | tf_op jit(solution)/shard_map/ppermute | solution.py:43
  26.8 3.7 %collective-permute-start.6 = (bf16[24,896]{1,0:T(8,128)(2,1)S(1)}, bf16[24,896]{1,0:T(8,128)(2,1)S(1)}, u32[]{:S(2)}, u32[]{:S(2)}) collective-permute-start(bf16[24,896]{1,0:T(8,128)(2,1)S(1)} %shard_map.80.refs_0_), channel_id=1, source_target_pairs={{0,24},{8,16},{16,8},{24,0},{1,25},{9,17},{17,9},{25,1},{2,26},{10... | collective-permute-start | bytes 129032 | tf_op jit(solution)/shard_map/ppermute | solution.py:43
  30.5 0.8 %collective-permute-start.4 = (bf16[24,896]{1,0:T(8,128)(2,1)S(1)}, bf16[24,896]{1,0:T(8,128)(2,1)S(1)}, u32[]{:S(2)}, u32[]{:S(2)}) collective-permute-start(bf16[24,896]{1,0:T(8,128)(2,1)S(1)} %shard_map.80.refs_0_), channel_id=1, source_target_pairs={{0,8},{8,0},{16,24},{24,16},{1,9},{9,1},{17,25},{25,17},{2,10},{10... | collective-permute-start | bytes 129032 | tf_op jit(solution)/shard_map/ppermute | solution.py:43
  31.3 1.4 %collective-permute-done.6.refs_3_ = bf16[24,896]{1,0:T(8,128)(2,1)S(1)} collective-permute-done((bf16[24,896]{1,0:T(8,128)(2,1)S(1)}, bf16[24,896]{1,0:T(8,128)(2,1)S(1)}, u32[]{:S(2)}, u32[]{:S(2)}) %collective-permute-start.6) | collective-permute-done | bytes 43040 | tf_op jit(solution)/shard_map/ppermute | solution.py:43
  32.7 2.7 %collective-permute-done.5.refs_2_ = bf16[24,896]{1,0:T(8,128)(2,1)S(1)} collective-permute-done((bf16[24,896]{1,0:T(8,128)(2,1)S(1)}, bf16[24,896]{1,0:T(8,128)(2,1)S(1)}, u32[]{:S(2)}, u32[]{:S(2)}) %collective-permute-start.5) | collective-permute-done | bytes 43040 | tf_op jit(solution)/shard_map/ppermute | solution.py:43
  35.4 0.6 shard_map.81.mine
  36.0 0.1 collective-permute-start.7
  36.1 1.3 %collective-permute-done.7.other = bf16[24,2048]{1,0:T(8,128)(2,1)S(1)} collective-permute-done((bf16[24,2048]{1,0:T(8,128)(2,1)S(1)}, bf16[24,2048]{1,0:T(8,128)(2,1)S(1)}, u32[]{:S(2)}, u32[]{:S(2)}) %collective-permute-start.7) | collective-permute-done | bytes 98336 | tf_op jit(solution)/shard_map/ppermute | solution.py:245
  37.4 0.8 %shard_map.82.refs_0_ = bf16[48,1024]{1,0:T(8,128)(2,1)S(1)} custom-call(bf16[24,2048]{1,0:T(8,128)(2,1)S(1)} %shard_map.81.mine, bf16[24,2048]{1,0:T(8,128)(2,1)S(1)} %collective-permute-done.7.other, bf16[2048,1024]{1,0:T(8,128)(2,1)S(1)} %copy-done.1), custom_call_target="tpu_custom_call" | custom-call | flops 201326592 | bytes 1048576 | tf_op jit(solution)/shard_map/pallas_call | solution.py:18
  38.2 1.5 %collective-permute-start.10 = (bf16[48,1024]{1,0:T(8,128)(2,1)S(1)}, bf16[48,1024]{1,0:T(8,128)(2,1)S(1)}, u32[]{:S(2)}, u32[]{:S(2)}) collective-permute-start(bf16[48,1024]{1,0:T(8,128)(2,1)S(1)} %shard_map.82.refs_0_), channel_id=1, source_target_pairs={{0,24},{8,16},{16,8},{24,0},{1,25},{9,17},{17,9},{25,1},{2,26},{10... | collective-permute-start | bytes 294920 | tf_op jit(solution)/shard_map/ppermute | solution.py:43
  39.8 0.6 collective-permute-start.9
  40.4 2.3 %collective-permute-start.8 = (bf16[48,1024]{1,0:T(8,128)(2,1)S(1)}, bf16[48,1024]{1,0:T(8,128)(2,1)S(1)}, u32[]{:S(2)}, u32[]{:S(2)}) collective-permute-start(bf16[48,1024]{1,0:T(8,128)(2,1)S(1)} %shard_map.82.refs_0_), channel_id=1, source_target_pairs={{0,8},{8,0},{16,24},{24,16},{1,9},{9,1},{17,25},{25,17},{2,10},{10... | collective-permute-start | bytes 294920 | tf_op jit(solution)/shard_map/ppermute | solution.py:43
  42.7 3.2 %collective-permute-done.10.refs_3_ = bf16[48,1024]{1,0:T(8,128)(2,1)S(1)} collective-permute-done((bf16[48,1024]{1,0:T(8,128)(2,1)S(1)}, bf16[48,1024]{1,0:T(8,128)(2,1)S(1)}, u32[]{:S(2)}, u32[]{:S(2)}) %collective-permute-start.10) | collective-permute-done | bytes 98336 | tf_op jit(solution)/shard_map/ppermute | solution.py:43
  45.9 3.9 %collective-permute-done.9.refs_2_ = bf16[48,1024]{1,0:T(8,128)(2,1)S(1)} collective-permute-done((bf16[48,1024]{1,0:T(8,128)(2,1)S(1)}, bf16[48,1024]{1,0:T(8,128)(2,1)S(1)}, u32[]{:S(2)}, u32[]{:S(2)}) %collective-permute-start.9) | collective-permute-done | bytes 98336 | tf_op jit(solution)/shard_map/ppermute | solution.py:43
  49.8 0.1 shard_map.83
  49.8 10.0 %all-gather.1 = bf16[384,1024]{1,0:T(8,128)(2,1)S(1)} all-gather(bf16[48,1024]{1,0:T(8,128)(2,1)S(1)} %shard_map.83), channel_id=3, replica_groups=mesh['dom'=4,'col'=8] {'col'}, dimensions={0}, use_global_device_ids=true | all-gather | bytes 884736 | tf_op jit(solution)/shard_map/all_gather | solution.py:259
  59.8 2.0 %shard_map.84 = (bf16[48,1024]{1,0:T(8,128)(2,1)S(1)}, bf16[6,8192]{1,0:T(8,128)(2,1)}) custom-call(s32[1,6]{1,0:T(1,128)S(1)} %copy-done.2, bf16[8,48,1024]{2,1,0:T(8,128)(2,1)S(1)} %bitcast.14, bf16[8,6,10240]{2,1,0:T(8,128)(2,1)S(1)} %all-gather.3.gathered, bf16[1024,768]{1,0:T(8,128)(2,1)S(1)} %bitcast.12), custom_call_target="tpu_custom_call" | custom-call | flops 75497472 | bytes 1048576 | tf_op jit(solution)/shard_map/pallas_call | solution.py:260
  61.8 9.8 %all-gather.2 = bf16[384,1024]{1,0:T(8,128)(2,1)S(1)} all-gather(bf16[48,1024]{1,0:T(8,128)(2,1)S(1)} %get-tuple-element.8), channel_id=4, replica_groups=mesh['dom'=4,'col'=8] {'col'}, dimensions={0}, use_global_device_ids=true | all-gather | bytes 884736 | tf_op jit(solution)/shard_map/all_gather | solution.py:279
  71.6 3.7 %shard_map.85 = bf16[48,1024]{1,0:T(8,128)(2,1)} custom-call(bf16[8,48,1024]{2,1,0:T(8,128)(2,1)S(1)} %bitcast.13, bf16[8192,1024]{1,0:T(8,128)(2,1)S(1)} %bitcast.10), custom_call_target="tpu_custom_call" | custom-call | flops 805306368 | bytes 1048576 | tf_op jit(solution)/shard_map/pallas_call | solution.py:18
  (18 shorter events, 0.1 us)
Async XLA Ops:
  0.6 15.0 %slice-start = ((s8[16777216]{0:T(1024)(128)(4,1)}), s8[4194304]{0:T(1024)(128)(4,1)S(1)}, s32[]{:S(2)}) async-start(s8[16777216]{0:T(1024)(128)(4,1)} %bitcast.7), calls=%async_computation | async-start | bytes 8388608
  0.6 15.0 %slice-start.1 = ((s8[16777216]{0:T(1024)(128)(4,1)}), s8[4194304]{0:T(1024)(128)(4,1)S(1)}, s32[]{:S(2)}) async-start(s8[16777216]{0:T(1024)(128)(4,1)} %bitcast.7), calls=%async_computation.1 | async-start | bytes 8388608
  0.7 15.0 %slice-start.2 = ((s8[16777216]{0:T(1024)(128)(4,1)}), s8[4194304]{0:T(1024)(128)(4,1)S(1)}, s32[]{:S(2)}) async-start(s8[16777216]{0:T(1024)(128)(4,1)} %bitcast.7), calls=%async_computation.2 | async-start | bytes 8388608
  0.7 14.9 %slice-start.3 = ((s8[16777216]{0:T(1024)(128)(4,1)}), s8[4194304]{0:T(1024)(128)(4,1)S(1)}, s32[]{:S(2)}) async-start(s8[16777216]{0:T(1024)(128)(4,1)} %bitcast.7), calls=%async_computation.3 | async-start | bytes 8388608
  0.7 14.9 %copy-start = (bf16[1,1024,768]{2,1,0:T(8,128)(2,1)S(1)}, bf16[1,1024,768]{2,1,0:T(8,128)(2,1)}, u32[]{:S(2)}) copy-start(bf16[1,1024,768]{2,1,0:T(8,128)(2,1)} %param.8) | copy-start | bytes 4718596
  15.6 8.3 %copy-start.2 = (s32[1,6]{1,0:T(1,128)S(1)}, s32[1,6]{1,0:T(1,128)}, u32[]{:S(2)}) copy-start(s32[1,6]{1,0:T(1,128)} %ids.1) | copy-start | bytes 76
  15.6 21.7 %copy-start.1 = (bf16[2048,1024]{1,0:T(8,128)(2,1)S(1)}, bf16[2048,1024]{1,0:T(8,128)(2,1)}, u32[]{:S(2)}) copy-start(bf16[2048,1024]{1,0:T(8,128)(2,1)} %inverse.1) | copy-start | bytes 12582916
  19.1 1.3 %collective-permute-start = (bf16[24,768]{1,0:T(8,128)(2,1)S(1)}, bf16[24,768]{1,0:T(8,128)(2,1)S(1)}, u32[]{:S(2)}, u32[]{:S(2)}) collective-permute-start(bf16[24,768]{1,0:T(8,128)(2,1)S(1)} %get-tuple-element.7), channel_id=1, source_target_pairs={{0,1},{1,0},{2,3},{3,2},{4,5},{5,4},{6,7},{7,6},{8,9},{9,8},{10,11... | collective-permute-start | bytes 110600 | tf_op jit(solution)/shard_map/ppermute | solution.py:230
  20.4 4.9 %collective-permute-start.3 = (bf16[24,768]{1,0:T(8,128)(2,1)S(1)}, bf16[24,768]{1,0:T(8,128)(2,1)S(1)}, u32[]{:S(2)}, u32[]{:S(2)}) collective-permute-start(bf16[24,768]{1,0:T(8,128)(2,1)S(1)} %shard_map.79.refs_0_), channel_id=1, source_target_pairs={{0,6},{1,7},{2,4},{3,5},{4,2},{5,3},{6,0},{7,1},{8,14},{9,15},{10,... | collective-permute-start | bytes 110600 | tf_op jit(solution)/shard_map/ppermute | solution.py:43
  21.9 4.0 %collective-permute-start.2 = (bf16[24,768]{1,0:T(8,128)(2,1)S(1)}, bf16[24,768]{1,0:T(8,128)(2,1)S(1)}, u32[]{:S(2)}, u32[]{:S(2)}) collective-permute-start(bf16[24,768]{1,0:T(8,128)(2,1)S(1)} %shard_map.79.refs_0_), channel_id=1, source_target_pairs={{0,4},{1,5},{2,6},{3,7},{4,0},{5,1},{6,2},{7,3},{8,12},{9,13},{10,... | collective-permute-start | bytes 110600 | tf_op jit(solution)/shard_map/ppermute | solution.py:43
  22.8 4.0 %collective-permute-start.1 = (bf16[24,768]{1,0:T(8,128)(2,1)S(1)}, bf16[24,768]{1,0:T(8,128)(2,1)S(1)}, u32[]{:S(2)}, u32[]{:S(2)}) collective-permute-start(bf16[24,768]{1,0:T(8,128)(2,1)S(1)} %shard_map.79.refs_0_), channel_id=1, source_target_pairs={{0,2},{1,3},{2,0},{3,1},{4,6},{5,7},{6,4},{7,5},{8,10},{9,11},{10,... | collective-permute-start | bytes 110600 | tf_op jit(solution)/shard_map/ppermute | solution.py:43
  26.8 5.9 %collective-permute-start.6 = (bf16[24,896]{1,0:T(8,128)(2,1)S(1)}, bf16[24,896]{1,0:T(8,128)(2,1)S(1)}, u32[]{:S(2)}, u32[]{:S(2)}) collective-permute-start(bf16[24,896]{1,0:T(8,128)(2,1)S(1)} %shard_map.80.refs_0_), channel_id=1, source_target_pairs={{0,24},{8,16},{16,8},{24,0},{1,25},{9,17},{17,9},{25,1},{2,26},{10... | collective-permute-start | bytes 129032 | tf_op jit(solution)/shard_map/ppermute | solution.py:43
  30.5 4.9 %collective-permute-start.5 = (bf16[24,896]{1,0:T(8,128)(2,1)S(1)}, bf16[24,896]{1,0:T(8,128)(2,1)S(1)}, u32[]{:S(2)}, u32[]{:S(2)}) collective-permute-start(bf16[24,896]{1,0:T(8,128)(2,1)S(1)} %shard_map.80.refs_0_), channel_id=1, source_target_pairs={{0,16},{8,24},{16,0},{24,8},{1,17},{9,25},{17,1},{25,9},{2,18},{10... | collective-permute-start | bytes 129032 | tf_op jit(solution)/shard_map/ppermute | solution.py:43
  30.5 4.9 %collective-permute-start.4 = (bf16[24,896]{1,0:T(8,128)(2,1)S(1)}, bf16[24,896]{1,0:T(8,128)(2,1)S(1)}, u32[]{:S(2)}, u32[]{:S(2)}) collective-permute-start(bf16[24,896]{1,0:T(8,128)(2,1)S(1)} %shard_map.80.refs_0_), channel_id=1, source_target_pairs={{0,8},{8,0},{16,24},{24,16},{1,9},{9,1},{17,25},{25,17},{2,10},{10... | collective-permute-start | bytes 129032 | tf_op jit(solution)/shard_map/ppermute | solution.py:43
  36.0 1.4 %collective-permute-start.7 = (bf16[24,2048]{1,0:T(8,128)(2,1)S(1)}, bf16[24,2048]{1,0:T(8,128)(2,1)S(1)}, u32[]{:S(2)}, u32[]{:S(2)}) collective-permute-start(bf16[24,2048]{1,0:T(8,128)(2,1)S(1)} %shard_map.81.mine), channel_id=1, source_target_pairs={{0,1},{1,0},{2,3},{3,2},{4,5},{5,4},{6,7},{7,6},{8,9},{9,8},{10,11... | collective-permute-start | bytes 294920 | tf_op jit(solution)/shard_map/ppermute | solution.py:245
  38.2 7.6 %collective-permute-start.10 = (bf16[48,1024]{1,0:T(8,128)(2,1)S(1)}, bf16[48,1024]{1,0:T(8,128)(2,1)S(1)}, u32[]{:S(2)}, u32[]{:S(2)}) collective-permute-start(bf16[48,1024]{1,0:T(8,128)(2,1)S(1)} %shard_map.82.refs_0_), channel_id=1, source_target_pairs={{0,24},{8,16},{16,8},{24,0},{1,25},{9,17},{17,9},{25,1},{2,26},{10... | collective-permute-start | bytes 294920 | tf_op jit(solution)/shard_map/ppermute | solution.py:43
  39.8 10.0 %collective-permute-start.9 = (bf16[48,1024]{1,0:T(8,128)(2,1)S(1)}, bf16[48,1024]{1,0:T(8,128)(2,1)S(1)}, u32[]{:S(2)}, u32[]{:S(2)}) collective-permute-start(bf16[48,1024]{1,0:T(8,128)(2,1)S(1)} %shard_map.82.refs_0_), channel_id=1, source_target_pairs={{0,16},{8,24},{16,0},{24,8},{1,17},{9,25},{17,1},{25,9},{2,18},{10... | collective-permute-start | bytes 294920 | tf_op jit(solution)/shard_map/ppermute | solution.py:43
  40.4 9.4 %collective-permute-start.8 = (bf16[48,1024]{1,0:T(8,128)(2,1)S(1)}, bf16[48,1024]{1,0:T(8,128)(2,1)S(1)}, u32[]{:S(2)}, u32[]{:S(2)}) collective-permute-start(bf16[48,1024]{1,0:T(8,128)(2,1)S(1)} %shard_map.82.refs_0_), channel_id=1, source_target_pairs={{0,8},{8,0},{16,24},{24,16},{1,9},{9,1},{17,25},{25,17},{2,10},{10... | collective-permute-start | bytes 294920 | tf_op jit(solution)/shard_map/ppermute | solution.py:43

commit v3 on v2

--- a/solution.py
+++ b/solution.py
@@ -6,6 +6,7 @@
 from jax.experimental import pallas as pl
 from jax.experimental.pallas import tpu as pltpu
 from jax.sharding import PartitionSpec as P
+
 
 LANES = 128
 CORES = 2
@@ -39,10 +40,10 @@
 
 def exchange(value, axis, stride=1):
     size = lax.axis_size(axis)
-    return [
-        lax.ppermute(value, axis, pairs_of(size, shift, stride))
-        for shift in range(1, size // stride)
-    ]
+    pieces = []
+    for shift in range(1, size // stride):
+        pieces.append(lax.ppermute(value, axis, pairs_of(size, shift, stride)))
+    return pieces
 
 
 def dot(left, right):
@@ -88,7 +89,7 @@
     out[...] = total.astype(BF16)
 
 
-def pack_kernel(block_count, *refs):
+def pack_kernel(*refs):
     ids, out = refs[-2], refs[-1]
     width = refs[0].shape[1]
     total = refs[0][...].astype(F32)
@@ -142,7 +143,7 @@
     out[...] = dot(reduced[...], inverse[...]).astype(BF16)
 
 
-def backward_kernel(block_size, ids, total, gathered, couple, out, solution, picked):
+def backward_kernel(block_size, ids, total, gathered, couple, out, picked):
     slabs, rows, columns = total.shape
     row_count = gathered.shape[1]
     own_columns = couple.shape[0]
@@ -172,6 +173,61 @@
         part = slice(slab * row_count, (slab + 1) * row_count)
         have = gathered[slab, :, pl.ds(start, own_columns)].astype(F32)
         out[part] = (have - correction[part]).astype(BF16)
+
+
+def stack_kernel(*refs):
+    out = refs[-1]
+    for index, ref in enumerate(refs[:-1]):
+        out[index] = ref[...]
+
+
+def unit_from(unit, shift, members):
+    if members & (members - 1) == 0:
+        return lax.bitwise_xor(unit, shift)
+    return lax.rem(unit + members - shift, members)
+
+
+def product_kernel(members, sources, inverse, carry, *refs):
+    out = refs[-1]
+    columns = refs[0].shape[-1]
+    col = lax.axis_index("col")
+    unit, core = lax.div(col, CORES), lax.rem(col, CORES)
+    total = None if carry is None else carry[...]
+    blocks = [ref for ref in refs[:-1] if len(ref.shape) == 2]
+    for ref in refs[:-1]:
+        if len(ref.shape) == 3:
+            blocks += [ref.at[index] for index in range(ref.shape[0])]
+    for block, (shift, other) in zip(blocks, sources):
+        owner = unit_from(unit, shift, members) * CORES + lax.rem(core + other, CORES)
+        start = pl.multiple_of(owner * columns, LANES)
+        term = dot(block[...], inverse[pl.ds(start, columns), :])
+        total = term if total is None else total + term
+    out[...] = total.astype(out.dtype)
+
+
+def product(members, sources, inverse, carry, blocks, dtype):
+    rows, columns = blocks[0].shape[-2:]
+    operands = [inverse] + ([] if carry is None else [carry]) + list(blocks)
+    kernel = functools.partial(product_kernel, members, sources)
+    if carry is None:
+        kernel = lambda inverse_ref, *refs: product_kernel(members, sources, inverse_ref, None, *refs)
+    return pl.pallas_call(
+        kernel,
+        out_shape=jax.ShapeDtypeStruct((rows, inverse.shape[1]), dtype),
+        in_specs=[WHOLE] * len(operands),
+        out_specs=WHOLE,
+        compiler_params=pltpu.CompilerParams(vmem_limit_bytes=8 * 2**20),
+        cost_estimate=pl.CostEstimate(
+            flops=2 * rows * columns * inverse.shape[1] * len(sources),
+            bytes_accessed=2**20,
+            transcendentals=0,
+        ),
+    )(*[pltpu.with_memory_space_constraint(operand, pltpu.VMEM) for operand in operands])
+
+
+def pick_kernel(row_count, total, solution):
+    slabs, rows, columns = total.shape
+    col = lax.axis_index("col")
     first = lax.rem(col, CORES) * (rows // CORES) + lax.div(col, CORES) * row_count
     pick_row = lax.broadcasted_iota(jnp.int32, (8, rows), 0)
     pick_place = lax.broadcasted_iota(jnp.int32, (8, rows), 1)
@@ -179,13 +235,6 @@
     for slab in range(slabs):
         chosen = dot(pick, total[slab])[:row_count]
         solution[:, slab * columns : (slab + 1) * columns] = chosen.astype(BF16)
-
-
-def last_kernel(every, inverse, out, rhs):
-    slabs, rows, columns = every.shape
-    for slab in range(slabs):
-        rhs[:, slab * columns : (slab + 1) * columns] = every[slab]
-    out[...] = dot(rhs[...], inverse[...]).astype(BF16)
 
 
 def per_device(rhs_interior, interior_inv, coupling, rhs_interface, block_ids, interface_inv):
@@ -219,6 +268,7 @@
     gathered = lax.all_gather(joined, "col", axis=0)
     ids_row = jnp.pad(block_ids, ((0, 0), (0, LANES - block_count)))
 
+    core_pairs = [(source, source ^ 1) for source in range(col_size)]
     keep, give = run(
         functools.partial(forward_kernel, half),
         [(half, local_count)] * 2,
@@ -227,10 +277,10 @@
         [pltpu.VMEM((rows, interior), BF16)],
         limit=12,
     )
-    other = lax.ppermute(give, "col", [(source, source ^ 1) for source in range(col_size)])
+    other = lax.ppermute(give, "col", core_pairs)
     (pair,) = run(add_kernel, [(half, local_count)], [keep, other], half * local_count)
     (packed,) = run(
-        functools.partial(pack_kernel, block_count),
+        pack_kernel,
         [(half, local_count + LANES)],
         [pair, *exchange(pair, "col", CORES), ids_row],
         half * local_count,
@@ -242,7 +292,7 @@
         rows * width * 64,
         limit=16,
     )
-    reduced_other = lax.ppermute(reduced, "col", [(source, source ^ 1) for source in range(col_size)])
+    reduced_other = lax.ppermute(reduced, "col", core_pairs)
     (part_solution,) = run(
         interface_kernel,
         [(rows, columns)],
@@ -257,14 +307,11 @@
         rows * columns,
     )
     every_total = lax.all_gather(total, "col", axis=0)
-    interior_rhs, solution = pl.pallas_call(
+    interior_rhs = pl.pallas_call(
         functools.partial(backward_kernel, block_size),
-        out_shape=[
-            jax.ShapeDtypeStruct((rows, own_columns), BF16),
-            jax.ShapeDtypeStruct((row_count, columns * col_size), BF16),
-        ],
+        out_shape=jax.ShapeDtypeStruct((rows, own_columns), BF16),
         in_specs=[pl.BlockSpec(memory_space=pltpu.SMEM)] + [WHOLE] * 3,
-        out_specs=[WHOLE] * 2,
+        out_specs=WHOLE,
         scratch_shapes=[pltpu.VMEM((rows, local_count), BF16)],
         compiler_params=pltpu.CompilerParams(vmem_limit_bytes=8 * 2**20),
         cost_estimate=pl.CostEstimate(
@@ -276,14 +323,22 @@
         pltpu.with_memory_space_constraint(gathered, pltpu.VMEM),
         pltpu.with_memory_space_constraint(couple, pltpu.VMEM),
     )
-    every_rhs = lax.all_gather(interior_rhs, "col", axis=0)
-    (result,) = run(
-        last_kernel,
-        [(rows, own_columns)],
-        [every_rhs, inverse],
-        2 * rows * own_columns * interior,
-        [pltpu.VMEM((rows, interior), BF16)],
-    )
+    members = col_size // CORES
+    far = exchange(interior_rhs, "col", CORES)
+    peer = lax.ppermute(interior_rhs, "col", core_pairs)
+    (solution,) = run(
+        functools.partial(pick_kernel, row_count),
+        [(row_count, columns * col_size)],
+        [every_total],
+        2 * 8 * rows * columns * col_size,
+    )
+    near = [interior_rhs, peer]
+    first_sum = product(members, [(0, 0), (0, 1)], inverse, None, near, F32)
+    (stacked,) = run(stack_kernel, [(members - 1, rows, own_columns)], far, rows * own_columns)
+    far_peer = lax.ppermute(stacked, "col", core_pairs)
+    shifts = range(1, members)
+    second_sum = product(members, [(k, 0) for k in shifts], inverse, first_sum, [stacked], F32)
+    result = product(members, [(k, 1) for k in shifts], inverse, second_sum, [far_peer], BF16)
     return (result[None], solution)
 
 

time: 75.5 us -> 75.1 us (level)
  blocking collectives: 33.6 us -> 23.8 us
  waiting for transfers between devices: 16.2 us -> 21.1 us
  starting transfers between devices: 13 us -> 17.1 us
    all_gather x1 -> x0, blocking collectives: 9.78 us -> none  [per_device(): every_rhs = lax.all_gather(interior_rhs, 'col', axis=0)]
    ppermute x11 -> x16, waiting for transfers between devices: 16.2 us -> 21.1 us  [the longest x12 18.6 us: exchange(): pieces.append(lax.ppermute(value, axis, pairs_of(size, shift, stride)))]
    ppermute x11 -> x16, starting transfers between devices: 13 us -> 17.1 us  [the longest x12 16 us: exchange(): pieces.append(lax.ppermute(value, axis, pairs_of(size, shift, stride)))]
    pallas_call x0 -> x3, Pallas kernels: none -> 3.89 us  [product(): pl.pallas_call(kernel, out_shape=jax.ShapeDtypeStruct((rows, inverse.shap...]
    pallas_call x7 -> x8, Pallas kernels: 8.62 us -> 5.85 us  [run(): pl.pallas_call(kernel, out_shape=[jax.ShapeDtypeStruct(shape, BF16) for s...]
    pallas_call x1, Pallas kernels: 1.97 us -> 1.2 us  [per_device(): pl.pallas_call(functools.partial(backward_kernel, block_size), out_shape=...]
  transfers between devices with their start and end apart: 11 -> 16, of which waited for: 9 -> 12; matrix products, arithmetic and copies ran while one was open for 0% -> 0% of each run, Pallas kernels for 0% -> 4%
where the time goes in v3:
time: 75.1 us; the launch traced here: 74.9 us
  blocking collectives  23.8 us (32%)
  waiting for transfers between devices  21.1 us (28%)
  starting transfers between devices  17.1 us (23%)
  Pallas kernels  12 us (16%)
  between operations  0.8 us (1%)
    ppermute x12, waiting for transfers between devices, exchange(): pieces.append(lax.ppermute(value, axis, pairs_of(size, shift, stride)))  18.6 us
    ppermute x12, starting transfers between devices, exchange(): pieces.append(lax.ppermute(value, axis, pairs_of(size, shift, stride)))  16 us
    all_gather x1, blocking collectives, per_device(): gathered = lax.all_gather(joined, 'col', axis=0)  13.8 us
    all_gather x1, blocking collectives, per_device(): every_total = lax.all_gather(total, 'col', axis=0)  10 us
    pallas_call x8, Pallas kernels, run(): pl.pallas_call(kernel, out_shape=[jax.ShapeDtypeStruct(shape, BF16) for s...  5.85 us
    pallas_call x3, Pallas kernels, product(): pl.pallas_call(kernel, out_shape=jax.ShapeDtypeStruct((rows, inverse.shap...  3.89 us
  transfers between devices with their start and end apart: 16, of which 12 were waited for; matrix products, arithmetic and copies ran while one was open for 0% of the time, Pallas kernels for 4%

profile of v3, /device:TPU:0, one launch (start us, length us, event | category | flops | bytes accessed | tf_op | source)
XLA Modules:
  0.0 74.9 jit_solution(12960308904870439036)
XLA Ops:
  0.7 1.1 %shard_map.77 = bf16[6,10240]{1,0:T(8,128)(2,1)S(1)} custom-call(bf16[6,8192]{1,0:T(8,128)(2,1)} %bitcast.18, bf16[6,2048]{1,0:T(8,128)(2,1)} %interface.1), custom_call_target="tpu_custom_call" | custom-call | flops 25769803776 | bytes 1048576 | tf_op jit(solution)/shard_map/pallas_call | solution.py:254
  1.8 13.8 %all-gather.2.gathered = bf16[8,6,10240]{2,1,0:T(8,128)(2,1)S(1)} all-gather(bf16[1,6,10240]{2,1,0:T(8,128)(2,1)S(1)} %bitcast.16), channel_id=2, replica_groups=mesh['dom'=4,'col'=8] {'col'}, dimensions={0}, use_global_device_ids=true | all-gather | bytes 1105920 | tf_op jit(solution)/shard_map/all_gather | solution.py:268
  15.7 3.4 %shard_map.78 = (bf16[24,768]{1,0:T(8,128)(2,1)S(1)}, bf16[24,768]{1,0:T(8,128)(2,1)S(1)}) custom-call(bf16[8,6,10240]{2,1,0:T(8,128)(2,1)S(1)} %all-gather.2.gathered, bf16[8192,1024]{1,0:T(8,128)(2,1)S(1)} %bitcast.8, bf16[1024,768]{1,0:T(8,128)(2,1)S(1)} %bitcast.14), custom_call_target="tpu_custom_call" | custom-call | flops 880803840 | bytes 1048576 | tf_op jit(solution)/shard_map/pallas_call | solution.py:19
  19.5 0.9 %collective-permute-done.refs_1_ = bf16[24,768]{1,0:T(8,128)(2,1)S(1)} collective-permute-done((bf16[24,768]{1,0:T(8,128)(2,1)S(1)}, bf16[24,768]{1,0:T(8,128)(2,1)S(1)}, u32[]{:S(2)}, u32[]{:S(2)}) %collective-permute-start) | collective-permute-done | bytes 36896 | tf_op jit(solution)/shard_map/ppermute | solution.py:280
  20.4 1.5 %collective-permute-start.3 = (bf16[24,768]{1,0:T(8,128)(2,1)S(1)}, bf16[24,768]{1,0:T(8,128)(2,1)S(1)}, u32[]{:S(2)}, u32[]{:S(2)}) collective-permute-start(bf16[24,768]{1,0:T(8,128)(2,1)S(1)} %shard_map.79.refs_0_), channel_id=1, source_target_pairs={{0,6},{1,7},{2,4},{3,5},{4,2},{5,3},{6,0},{7,1},{8,14},{9,15},{10,... | collective-permute-start | bytes 110600 | tf_op jit(solution)/shard_map/ppermute | solution.py:45
  21.9 0.9 %collective-permute-start.2 = (bf16[24,768]{1,0:T(8,128)(2,1)S(1)}, bf16[24,768]{1,0:T(8,128)(2,1)S(1)}, u32[]{:S(2)}, u32[]{:S(2)}) collective-permute-start(bf16[24,768]{1,0:T(8,128)(2,1)S(1)} %shard_map.79.refs_0_), channel_id=1, source_target_pairs={{0,4},{1,5},{2,6},{3,7},{4,0},{5,1},{6,2},{7,3},{8,12},{9,13},{10,... | collective-permute-start | bytes 110600 | tf_op jit(solution)/shard_map/ppermute | solution.py:45
  22.8 1.1 %collective-permute-start.1 = (bf16[24,768]{1,0:T(8,128)(2,1)S(1)}, bf16[24,768]{1,0:T(8,128)(2,1)S(1)}, u32[]{:S(2)}, u32[]{:S(2)}) collective-permute-start(bf16[24,768]{1,0:T(8,128)(2,1)S(1)} %shard_map.79.refs_0_), channel_id=1, source_target_pairs={{0,2},{1,3},{2,0},{3,1},{4,6},{5,7},{6,4},{7,5},{8,10},{9,11},{10,... | collective-permute-start | bytes 110600 | tf_op jit(solution)/shard_map/ppermute | solution.py:45
  24.0 1.4 %collective-permute-done.3.refs_3_ = bf16[24,768]{1,0:T(8,128)(2,1)S(1)} collective-permute-done((bf16[24,768]{1,0:T(8,128)(2,1)S(1)}, bf16[24,768]{1,0:T(8,128)(2,1)S(1)}, u32[]{:S(2)}, u32[]{:S(2)}) %collective-permute-start.3) | collective-permute-done | bytes 36896 | tf_op jit(solution)/shard_map/ppermute | solution.py:45
  25.9 0.9 %collective-permute-done.1.refs_1_ = bf16[24,768]{1,0:T(8,128)(2,1)S(1)} collective-permute-done((bf16[24,768]{1,0:T(8,128)(2,1)S(1)}, bf16[24,768]{1,0:T(8,128)(2,1)S(1)}, u32[]{:S(2)}, u32[]{:S(2)}) %collective-permute-start.1) | collective-permute-done | bytes 36896 | tf_op jit(solution)/shard_map/ppermute | solution.py:45
  26.8 3.7 %collective-permute-start.6 = (bf16[24,896]{1,0:T(8,128)(2,1)S(1)}, bf16[24,896]{1,0:T(8,128)(2,1)S(1)}, u32[]{:S(2)}, u32[]{:S(2)}) collective-permute-start(bf16[24,896]{1,0:T(8,128)(2,1)S(1)} %shard_map.80.refs_0_), channel_id=1, source_target_pairs={{0,24},{8,16},{16,8},{24,0},{1,25},{9,17},{17,9},{25,1},{2,26},{10... | collective-permute-start | bytes 129032 | tf_op jit(solution)/shard_map/ppermute | solution.py:45
  30.5 0.8 %collective-permute-start.4 = (bf16[24,896]{1,0:T(8,128)(2,1)S(1)}, bf16[24,896]{1,0:T(8,128)(2,1)S(1)}, u32[]{:S(2)}, u32[]{:S(2)}) collective-permute-start(bf16[24,896]{1,0:T(8,128)(2,1)S(1)} %shard_map.80.refs_0_), channel_id=1, source_target_pairs={{0,8},{8,0},{16,24},{24,16},{1,9},{9,1},{17,25},{25,17},{2,10},{10... | collective-permute-start | bytes 129032 | tf_op jit(solution)/shard_map/ppermute | solution.py:45
  31.3 1.4 %collective-permute-done.6.refs_3_ = bf16[24,896]{1,0:T(8,128)(2,1)S(1)} collective-permute-done((bf16[24,896]{1,0:T(8,128)(2,1)S(1)}, bf16[24,896]{1,0:T(8,128)(2,1)S(1)}, u32[]{:S(2)}, u32[]{:S(2)}) %collective-permute-start.6) | collective-permute-done | bytes 43040 | tf_op jit(solution)/shard_map/ppermute | solution.py:45
  32.7 2.7 %collective-permute-done.5.refs_2_ = bf16[24,896]{1,0:T(8,128)(2,1)S(1)} collective-permute-done((bf16[24,896]{1,0:T(8,128)(2,1)S(1)}, bf16[24,896]{1,0:T(8,128)(2,1)S(1)}, u32[]{:S(2)}, u32[]{:S(2)}) %collective-permute-start.5) | collective-permute-done | bytes 43040 | tf_op jit(solution)/shard_map/ppermute | solution.py:45
  35.4 0.6 shard_map.81.mine
  36.1 1.3 %collective-permute-done.7.other = bf16[24,2048]{1,0:T(8,128)(2,1)S(1)} collective-permute-done((bf16[24,2048]{1,0:T(8,128)(2,1)S(1)}, bf16[24,2048]{1,0:T(8,128)(2,1)S(1)}, u32[]{:S(2)}, u32[]{:S(2)}) %collective-permute-start.7) | collective-permute-done | bytes 98336 | tf_op jit(solution)/shard_map/ppermute | solution.py:295
  37.4 0.8 %shard_map.82.refs_0_ = bf16[48,1024]{1,0:T(8,128)(2,1)S(1)} custom-call(bf16[24,2048]{1,0:T(8,128)(2,1)S(1)} %shard_map.81.mine, bf16[24,2048]{1,0:T(8,128)(2,1)S(1)} %collective-permute-done.7.other, bf16[2048,1024]{1,0:T(8,128)(2,1)S(1)} %copy-done.1), custom_call_target="tpu_custom_call" | custom-call | flops 201326592 | bytes 1048576 | tf_op jit(solution)/shard_map/pallas_call | solution.py:19
  38.2 1.5 %collective-permute-start.10 = (bf16[48,1024]{1,0:T(8,128)(2,1)S(1)}, bf16[48,1024]{1,0:T(8,128)(2,1)S(1)}, u32[]{:S(2)}, u32[]{:S(2)}) collective-permute-start(bf16[48,1024]{1,0:T(8,128)(2,1)S(1)} %shard_map.82.refs_0_), channel_id=1, source_target_pairs={{0,24},{8,16},{16,8},{24,0},{1,25},{9,17},{17,9},{25,1},{2,26},{10... | collective-permute-start | bytes 294920 | tf_op jit(solution)/shard_map/ppermute | solution.py:45
  39.8 0.6 collective-permute-start.9
  40.4 2.3 %collective-permute-start.8 = (bf16[48,1024]{1,0:T(8,128)(2,1)S(1)}, bf16[48,1024]{1,0:T(8,128)(2,1)S(1)}, u32[]{:S(2)}, u32[]{:S(2)}) collective-permute-start(bf16[48,1024]{1,0:T(8,128)(2,1)S(1)} %shard_map.82.refs_0_), channel_id=1, source_target_pairs={{0,8},{8,0},{16,24},{24,16},{1,9},{9,1},{17,25},{25,17},{2,10},{10... | collective-permute-start | bytes 294920 | tf_op jit(solution)/shard_map/ppermute | solution.py:45
  42.7 3.2 %collective-permute-done.10.refs_3_ = bf16[48,1024]{1,0:T(8,128)(2,1)S(1)} collective-permute-done((bf16[48,1024]{1,0:T(8,128)(2,1)S(1)}, bf16[48,1024]{1,0:T(8,128)(2,1)S(1)}, u32[]{:S(2)}, u32[]{:S(2)}) %collective-permute-start.10) | collective-permute-done | bytes 98336 | tf_op jit(solution)/shard_map/ppermute | solution.py:45
  45.9 3.9 %collective-permute-done.9.refs_2_ = bf16[48,1024]{1,0:T(8,128)(2,1)S(1)} collective-permute-done((bf16[48,1024]{1,0:T(8,128)(2,1)S(1)}, bf16[48,1024]{1,0:T(8,128)(2,1)S(1)}, u32[]{:S(2)}, u32[]{:S(2)}) %collective-permute-start.9) | collective-permute-done | bytes 98336 | tf_op jit(solution)/shard_map/ppermute | solution.py:45
  49.8 10.0 %all-gather.1 = bf16[384,1024]{1,0:T(8,128)(2,1)S(1)} all-gather(bf16[48,1024]{1,0:T(8,128)(2,1)S(1)} %shard_map.83), channel_id=3, replica_groups=mesh['dom'=4,'col'=8] {'col'}, dimensions={0}, use_global_device_ids=true | all-gather | bytes 884736 | tf_op jit(solution)/shard_map/all_gather | solution.py:309
  59.8 1.2 %shard_map.84.refs_0_ = bf16[48,1024]{1,0:T(8,128)(2,1)S(1)} custom-call(s32[1,6]{1,0:T(1,128)S(1)} %copy-done.2, bf16[8,48,1024]{2,1,0:T(8,128)(2,1)S(1)} %bitcast.12, bf16[8,6,10240]{2,1,0:T(8,128)(2,1)S(1)} %all-gather.2.gathered, bf16[1024,768]{1,0:T(8,128)(2,1)S(1)} %bitcast.15), custom_call_target="tpu_custom_call" | custom-call | flops 75497472 | bytes 1048576 | tf_op jit(solution)/shard_map/pallas_call | solution.py:310
  61.0 1.5 %collective-permute-start.14 = (bf16[48,1024]{1,0:T(8,128)(2,1)S(1)}, bf16[48,1024]{1,0:T(8,128)(2,1)S(1)}, u32[]{:S(2)}, u32[]{:S(2)}) collective-permute-start(bf16[48,1024]{1,0:T(8,128)(2,1)S(1)} %shard_map.84.refs_0_), channel_id=1, source_target_pairs={{0,6},{1,7},{2,4},{3,5},{4,2},{5,3},{6,0},{7,1},{8,14},{9,15},{10,... | collective-permute-start | bytes 294920 | tf_op jit(solution)/shard_map/ppermute | solution.py:45
  62.6 0.9 %collective-permute-start.13 = (bf16[48,1024]{1,0:T(8,128)(2,1)S(1)}, bf16[48,1024]{1,0:T(8,128)(2,1)S(1)}, u32[]{:S(2)}, u32[]{:S(2)}) collective-permute-start(bf16[48,1024]{1,0:T(8,128)(2,1)S(1)} %shard_map.84.refs_0_), channel_id=1, source_target_pairs={{0,4},{1,5},{2,6},{3,7},{4,0},{5,1},{6,2},{7,3},{8,12},{9,13},{10,... | collective-permute-start | bytes 294920 | tf_op jit(solution)/shard_map/ppermute | solution.py:45
  63.5 1.1 %collective-permute-start.12 = (bf16[48,1024]{1,0:T(8,128)(2,1)S(1)}, bf16[48,1024]{1,0:T(8,128)(2,1)S(1)}, u32[]{:S(2)}, u32[]{:S(2)}) collective-permute-start(bf16[48,1024]{1,0:T(8,128)(2,1)S(1)} %shard_map.84.refs_0_), channel_id=1, source_target_pairs={{0,2},{1,3},{2,0},{3,1},{4,6},{5,7},{6,4},{7,5},{8,10},{9,11},{10,... | collective-permute-start | bytes 294920 | tf_op jit(solution)/shard_map/ppermute | solution.py:45
  64.6 3.1 %collective-permute-done.14.refs_2_ = bf16[48,1024]{1,0:T(8,128)(2,1)S(1)} collective-permute-done((bf16[48,1024]{1,0:T(8,128)(2,1)S(1)}, bf16[48,1024]{1,0:T(8,128)(2,1)S(1)}, u32[]{:S(2)}, u32[]{:S(2)}) %collective-permute-start.14) | collective-permute-done | bytes 98336 | tf_op jit(solution)/shard_map/ppermute | solution.py:45
  67.7 1.5 %collective-permute-done.13.refs_1_ = bf16[48,1024]{1,0:T(8,128)(2,1)S(1)} collective-permute-done((bf16[48,1024]{1,0:T(8,128)(2,1)S(1)}, bf16[48,1024]{1,0:T(8,128)(2,1)S(1)}, u32[]{:S(2)}, u32[]{:S(2)}) %collective-permute-start.13) | collective-permute-done | bytes 98336 | tf_op jit(solution)/shard_map/ppermute | solution.py:45
  69.8 0.9 %shard_map.89 = bf16[6,8192]{1,0:T(8,128)(2,1)} custom-call(bf16[8,48,1024]{2,1,0:T(8,128)(2,1)S(1)} %bitcast.13), custom_call_target="tpu_custom_call" | custom-call | flops 6291456 | bytes 1048576 | tf_op jit(solution)/shard_map/pallas_call | solution.py:19
  71.0 0.8 %shard_map.85.carry = f32[48,1024]{1,0:T(8,128)S(1)} custom-call(bf16[8192,1024]{1,0:T(8,128)(2,1)S(1)} %bitcast.9, bf16[48,1024]{1,0:T(8,128)(2,1)S(1)} %shard_map.84.refs_0_, bf16[48,1024]{1,0:T(8,128)(2,1)S(1)} %collective-permute-done.11.refs_1_), custom_call_target="tpu_custom_call" | custom-call | flops 201326592 | bytes 1048576 | tf_op jit(solution)/shard_map/pallas_call | solution.py:214
  71.8 1.2 %shard_map.87.carry = f32[48,1024]{1,0:T(8,128)S(1)} custom-call(bf16[8192,1024]{1,0:T(8,128)(2,1)S(1)} %bitcast.10, f32[48,1024]{1,0:T(8,128)S(1)} %shard_map.85.carry, bf16[3,48,1024]{2,1,0:T(8,128)(2,1)S(1)} %shard_map.86.refs_0_), custom_call_target="tpu_custom_call" | custom-call | flops 301989888 | bytes 1048576 | tf_op jit(solution)/shard_map/pallas_call | solution.py:214
  73.0 1.9 %shard_map.88 = bf16[48,1024]{1,0:T(8,128)(2,1)} custom-call(bf16[8192,1024]{1,0:T(8,128)(2,1)S(1)} %bitcast.11, f32[48,1024]{1,0:T(8,128)S(1)} %shard_map.87.carry, bf16[3,48,1024]{2,1,0:T(8,128)(2,1)S(1)} %collective-permute-done.15.refs_0_), custom_call_target="tpu_custom_call" | custom-call | flops 301989888 | bytes 1048576 | tf_op jit(solution)/shard_map/pallas_call | solution.py:214
  (31 shorter events, 2.1 us)
Async XLA Ops:
  0.6 15.0 %slice-start = ((s8[16777216]{0:T(1024)(128)(4,1)}), s8[4194304]{0:T(1024)(128)(4,1)S(1)}, s32[]{:S(2)}) async-start(s8[16777216]{0:T(1024)(128)(4,1)} %bitcast.6), calls=%async_computation | async-start | bytes 8388608
  0.6 15.0 %slice-start.1 = ((s8[16777216]{0:T(1024)(128)(4,1)}), s8[4194304]{0:T(1024)(128)(4,1)S(1)}, s32[]{:S(2)}) async-start(s8[16777216]{0:T(1024)(128)(4,1)} %bitcast.6), calls=%async_computation.1 | async-start | bytes 8388608
  0.7 15.0 %slice-start.2 = ((s8[16777216]{0:T(1024)(128)(4,1)}), s8[4194304]{0:T(1024)(128)(4,1)S(1)}, s32[]{:S(2)}) async-start(s8[16777216]{0:T(1024)(128)(4,1)} %bitcast.6), calls=%async_computation.2 | async-start | bytes 8388608
  0.7 14.9 %slice-start.3 = ((s8[16777216]{0:T(1024)(128)(4,1)}), s8[4194304]{0:T(1024)(128)(4,1)S(1)}, s32[]{:S(2)}) async-start(s8[16777216]{0:T(1024)(128)(4,1)} %bitcast.6), calls=%async_computation.3 | async-start | bytes 8388608
  0.7 14.9 %copy-start = (bf16[1,1024,768]{2,1,0:T(8,128)(2,1)S(1)}, bf16[1,1024,768]{2,1,0:T(8,128)(2,1)}, u32[]{:S(2)}) copy-start(bf16[1,1024,768]{2,1,0:T(8,128)(2,1)} %param.8) | copy-start | bytes 4718596
  15.6 8.3 %copy-start.2 = (s32[1,6]{1,0:T(1,128)S(1)}, s32[1,6]{1,0:T(1,128)}, u32[]{:S(2)}) copy-start(s32[1,6]{1,0:T(1,128)} %ids.1) | copy-start | bytes 76
  15.6 21.7 %copy-start.1 = (bf16[2048,1024]{1,0:T(8,128)(2,1)S(1)}, bf16[2048,1024]{1,0:T(8,128)(2,1)}, u32[]{:S(2)}) copy-start(bf16[2048,1024]{1,0:T(8,128)(2,1)} %inverse.1) | copy-start | bytes 12582916
  19.1 1.3 %collective-permute-start = (bf16[24,768]{1,0:T(8,128)(2,1)S(1)}, bf16[24,768]{1,0:T(8,128)(2,1)S(1)}, u32[]{:S(2)}, u32[]{:S(2)}) collective-permute-start(bf16[24,768]{1,0:T(8,128)(2,1)S(1)} %get-tuple-element.5), channel_id=1, source_target_pairs={{0,1},{1,0},{2,3},{3,2},{4,5},{5,4},{6,7},{7,6},{8,9},{9,8},{10,11... | collective-permute-start | bytes 110600 | tf_op jit(solution)/shard_map/ppermute | solution.py:280
  20.4 4.9 %collective-permute-start.3 = (bf16[24,768]{1,0:T(8,128)(2,1)S(1)}, bf16[24,768]{1,0:T(8,128)(2,1)S(1)}, u32[]{:S(2)}, u32[]{:S(2)}) collective-permute-start(bf16[24,768]{1,0:T(8,128)(2,1)S(1)} %shard_map.79.refs_0_), channel_id=1, source_target_pairs={{0,6},{1,7},{2,4},{3,5},{4,2},{5,3},{6,0},{7,1},{8,14},{9,15},{10,... | collective-permute-start | bytes 110600 | tf_op jit(solution)/shard_map/ppermute | solution.py:45
  21.9 4.0 %collective-permute-start.2 = (bf16[24,768]{1,0:T(8,128)(2,1)S(1)}, bf16[24,768]{1,0:T(8,128)(2,1)S(1)}, u32[]{:S(2)}, u32[]{:S(2)}) collective-permute-start(bf16[24,768]{1,0:T(8,128)(2,1)S(1)} %shard_map.79.refs_0_), channel_id=1, source_target_pairs={{0,4},{1,5},{2,6},{3,7},{4,0},{5,1},{6,2},{7,3},{8,12},{9,13},{10,... | collective-permute-start | bytes 110600 | tf_op jit(solution)/shard_map/ppermute | solution.py:45
  22.8 4.0 %collective-permute-start.1 = (bf16[24,768]{1,0:T(8,128)(2,1)S(1)}, bf16[24,768]{1,0:T(8,128)(2,1)S(1)}, u32[]{:S(2)}, u32[]{:S(2)}) collective-permute-start(bf16[24,768]{1,0:T(8,128)(2,1)S(1)} %shard_map.79.refs_0_), channel_id=1, source_target_pairs={{0,2},{1,3},{2,0},{3,1},{4,6},{5,7},{6,4},{7,5},{8,10},{9,11},{10,... | collective-permute-start | bytes 110600 | tf_op jit(solution)/shard_map/ppermute | solution.py:45
  26.8 5.9 %collective-permute-start.6 = (bf16[24,896]{1,0:T(8,128)(2,1)S(1)}, bf16[24,896]{1,0:T(8,128)(2,1)S(1)}, u32[]{:S(2)}, u32[]{:S(2)}) collective-permute-start(bf16[24,896]{1,0:T(8,128)(2,1)S(1)} %shard_map.80.refs_0_), channel_id=1, source_target_pairs={{0,24},{8,16},{16,8},{24,0},{1,25},{9,17},{17,9},{25,1},{2,26},{10... | collective-permute-start | bytes 129032 | tf_op jit(solution)/shard_map/ppermute | solution.py:45
  30.5 4.9 %collective-permute-start.5 = (bf16[24,896]{1,0:T(8,128)(2,1)S(1)}, bf16[24,896]{1,0:T(8,128)(2,1)S(1)}, u32[]{:S(2)}, u32[]{:S(2)}) collective-permute-start(bf16[24,896]{1,0:T(8,128)(2,1)S(1)} %shard_map.80.refs_0_), channel_id=1, source_target_pairs={{0,16},{8,24},{16,0},{24,8},{1,17},{9,25},{17,1},{25,9},{2,18},{10... | collective-permute-start | bytes 129032 | tf_op jit(solution)/shard_map/ppermute | solution.py:45
  30.5 4.9 %collective-permute-start.4 = (bf16[24,896]{1,0:T(8,128)(2,1)S(1)}, bf16[24,896]{1,0:T(8,128)(2,1)S(1)}, u32[]{:S(2)}, u32[]{:S(2)}) collective-permute-start(bf16[24,896]{1,0:T(8,128)(2,1)S(1)} %shard_map.80.refs_0_), channel_id=1, source_target_pairs={{0,8},{8,0},{16,24},{24,16},{1,9},{9,1},{17,25},{25,17},{2,10},{10... | collective-permute-start | bytes 129032 | tf_op jit(solution)/shard_map/ppermute | solution.py:45
  36.0 1.4 %collective-permute-start.7 = (bf16[24,2048]{1,0:T(8,128)(2,1)S(1)}, bf16[24,2048]{1,0:T(8,128)(2,1)S(1)}, u32[]{:S(2)}, u32[]{:S(2)}) collective-permute-start(bf16[24,2048]{1,0:T(8,128)(2,1)S(1)} %shard_map.81.mine), channel_id=1, source_target_pairs={{0,1},{1,0},{2,3},{3,2},{4,5},{5,4},{6,7},{7,6},{8,9},{9,8},{10,11... | collective-permute-start | bytes 294920 | tf_op jit(solution)/shard_map/ppermute | solution.py:295
  38.2 7.6 %collective-permute-start.10 = (bf16[48,1024]{1,0:T(8,128)(2,1)S(1)}, bf16[48,1024]{1,0:T(8,128)(2,1)S(1)}, u32[]{:S(2)}, u32[]{:S(2)}) collective-permute-start(bf16[48,1024]{1,0:T(8,128)(2,1)S(1)} %shard_map.82.refs_0_), channel_id=1, source_target_pairs={{0,24},{8,16},{16,8},{24,0},{1,25},{9,17},{17,9},{25,1},{2,26},{10... | collective-permute-start | bytes 294920 | tf_op jit(solution)/shard_map/ppermute | solution.py:45
  39.8 10.0 %collective-permute-start.9 = (bf16[48,1024]{1,0:T(8,128)(2,1)S(1)}, bf16[48,1024]{1,0:T(8,128)(2,1)S(1)}, u32[]{:S(2)}, u32[]{:S(2)}) collective-permute-start(bf16[48,1024]{1,0:T(8,128)(2,1)S(1)} %shard_map.82.refs_0_), channel_id=1, source_target_pairs={{0,16},{8,24},{16,0},{24,8},{1,17},{9,25},{17,1},{25,9},{2,18},{10... | collective-permute-start | bytes 294920 | tf_op jit(solution)/shard_map/ppermute | solution.py:45
  40.4 9.4 %collective-permute-start.8 = (bf16[48,1024]{1,0:T(8,128)(2,1)S(1)}, bf16[48,1024]{1,0:T(8,128)(2,1)S(1)}, u32[]{:S(2)}, u32[]{:S(2)}) collective-permute-start(bf16[48,1024]{1,0:T(8,128)(2,1)S(1)} %shard_map.82.refs_0_), channel_id=1, source_target_pairs={{0,8},{8,0},{16,24},{24,16},{1,9},{9,1},{17,25},{25,17},{2,10},{10... | collective-permute-start | bytes 294920 | tf_op jit(solution)/shard_map/ppermute | solution.py:45
  61.0 6.6 %collective-permute-start.14 = (bf16[48,1024]{1,0:T(8,128)(2,1)S(1)}, bf16[48,1024]{1,0:T(8,128)(2,1)S(1)}, u32[]{:S(2)}, u32[]{:S(2)}) collective-permute-start(bf16[48,1024]{1,0:T(8,128)(2,1)S(1)} %shard_map.84.refs_0_), channel_id=1, source_target_pairs={{0,6},{1,7},{2,4},{3,5},{4,2},{5,3},{6,0},{7,1},{8,14},{9,15},{10,... | collective-permute-start | bytes 294920 | tf_op jit(solution)/shard_map/ppermute | solution.py:45
  62.6 6.6 %collective-permute-start.13 = (bf16[48,1024]{1,0:T(8,128)(2,1)S(1)}, bf16[48,1024]{1,0:T(8,128)(2,1)S(1)}, u32[]{:S(2)}, u32[]{:S(2)}) collective-permute-start(bf16[48,1024]{1,0:T(8,128)(2,1)S(1)} %shard_map.84.refs_0_), channel_id=1, source_target_pairs={{0,4},{1,5},{2,6},{3,7},{4,0},{5,1},{6,2},{7,3},{8,12},{9,13},{10,... | collective-permute-start | bytes 294920 | tf_op jit(solution)/shard_map/ppermute | solution.py:45
  63.5 5.7 %collective-permute-start.12 = (bf16[48,1024]{1,0:T(8,128)(2,1)S(1)}, bf16[48,1024]{1,0:T(8,128)(2,1)S(1)}, u32[]{:S(2)}, u32[]{:S(2)}) collective-permute-start(bf16[48,1024]{1,0:T(8,128)(2,1)S(1)} %shard_map.84.refs_0_), channel_id=1, source_target_pairs={{0,2},{1,3},{2,0},{3,1},{4,6},{5,7},{6,4},{7,5},{8,10},{9,11},{10,... | collective-permute-start | bytes 294920 | tf_op jit(solution)/shard_map/ppermute | solution.py:45
  69.2 3.8 %collective-permute-start.15 = (bf16[3,48,1024]{2,1,0:T(8,128)(2,1)S(1)}, bf16[3,48,1024]{2,1,0:T(8,128)(2,1)S(1)}, u32[]{:S(2)}, u32[]{:S(2)}) collective-permute-start(bf16[3,48,1024]{2,1,0:T(8,128)(2,1)S(1)} %shard_map.86.refs_0_), channel_id=1, source_target_pairs={{0,1},{1,0},{2,3},{3,2},{4,5},{5,4},{6,7},{7,6},{8,9},{9,8},{10,11... | collective-permute-start | bytes 884744 | tf_op jit(solution)/shard_map/ppermute | solution.py:338
  69.3 1.7 %collective-permute-start.11 = (bf16[48,1024]{1,0:T(8,128)(2,1)S(1)}, bf16[48,1024]{1,0:T(8,128)(2,1)S(1)}, u32[]{:S(2)}, u32[]{:S(2)}) collective-permute-start(bf16[48,1024]{1,0:T(8,128)(2,1)S(1)} %shard_map.84.refs_0_), channel_id=1, source_target_pairs={{0,1},{1,0},{2,3},{3,2},{4,5},{5,4},{6,7},{7,6},{8,9},{9,8},{10,11... | collective-permute-start | bytes 294920 | tf_op jit(solution)/shard_map/ppermute | solution.py:328

commit v4 on v3

--- a/solution.py
+++ b/solution.py
@@ -27,14 +27,13 @@
     )(*[pltpu.with_memory_space_constraint(operand, pltpu.VMEM) for operand in operands])
 
 
-def pairs_of(size, shift, stride=1):
+def pairs_of(size, shift, stride):
     members = size // stride
     xor = members & (members - 1) == 0
     pairs = []
-    for source in range(size):
-        unit, rest = divmod(source, stride)
+    for unit in range(members):
         target = unit ^ shift if xor else (unit + shift) % members
-        pairs.append((source, target * stride + rest))
+        pairs += [(unit * stride + lane, target * stride + lane) for lane in range(stride)]
     return pairs
 
 
@@ -50,25 +49,25 @@
     return jnp.dot(left, right, preferred_element_type=F32)
 
 
-def forward_kernel(half_rows, gathered, inverse, couple, keep, give, rhs):
+def forward_kernel(gathered, inverse, couple, keep, give, rhs):
     slabs, row_count, _ = gathered.shape
     interior = inverse.shape[0]
-    order = [slab for core in range(CORES) for slab in range(core, slabs, CORES)]
-    for place, slab in enumerate(order):
-        rhs[place * row_count : (place + 1) * row_count, :] = gathered[slab, :, :interior]
+    for slab in range(slabs):
+        rhs[slab * row_count : (slab + 1) * row_count, :] = gathered[slab, :, :interior]
     step = dot(rhs[...], inverse[...]).astype(BF16)
     part = dot(step, couple[...]).astype(BF16)
+    half = keep.shape[0]
     core = lax.rem(lax.axis_index("col"), CORES)
 
     @pl.when(core == 0)
     def _():
-        keep[...] = part[:half_rows]
-        give[...] = part[half_rows:]
+        keep[...] = part[:half]
+        give[...] = part[half:]
 
     @pl.when(core == 1)
     def _():
-        keep[...] = part[half_rows:]
-        give[...] = part[:half_rows]
+        keep[...] = part[half:]
+        give[...] = part[:half]
 
 
 def join_kernel(local, interface, out, sems):
@@ -99,80 +98,80 @@
     out[:, width:] = jnp.broadcast_to(ids[...].astype(F32), (out.shape[0], LANES)).astype(BF16)
 
 
-def place_kernel(block_count, block_size, gathered, *refs):
+def rows_kernel(gathered, interface_rows, own):
+    slabs, row_count, total = gathered.shape
+    interior = total - interface_rows.shape[1]
+    own_columns = own.shape[1]
+    col = lax.axis_index("col")
+    start = pl.multiple_of(col * own_columns, LANES)
+    half = slabs // CORES
+    base = lax.rem(col, CORES) * half
+    for slab in range(slabs):
+        part = slice(slab * row_count, (slab + 1) * row_count)
+        own[part] = gathered[slab, :, pl.ds(start, own_columns)]
+        if slab < half:
+            interface_rows[part] = gathered[base + slab, :, interior:]
+
+
+def turn_kernel(couple, out):
+    out[...] = couple[...].T
+
+
+def place_kernel(block_count, block_size, interface_rows, *refs):
     pieces, out = refs[:-1], refs[-1]
-    row_count = gathered.shape[1]
     rows, width = out.shape
-    interior = gathered.shape[2] - width
-    core = lax.rem(lax.axis_index("col"), CORES)
-    base = (lax.axis_index("dom") * (width // block_size)).astype(F32)
+    targets = width // block_size
+    base = (lax.axis_index("dom") * targets).astype(F32)
     span = block_count * block_size
-    ids = []
+    tile = 8
+    names = []
     for piece in pieces:
-        tail = piece[:, span:].astype(F32) - base
+        tail = piece[:tile, span:].astype(F32) - base
         for block in range(block_count):
-            ids.append(jnp.broadcast_to(tail[:, block : block + 1], (rows, block_size)))
-    for target in range(width // block_size):
+            names.append(jnp.broadcast_to(tail[:, block : block + 1], (tile, block_size)))
+    for target in range(targets):
         lanes = slice(target * block_size, (target + 1) * block_size)
-        total = jnp.zeros((rows, block_size), F32)
-        for index, name in enumerate(ids):
+        have = [
+            interface_rows[row : row + tile, lanes].astype(F32) for row in range(0, rows, tile)
+        ]
+        for index, name in enumerate(names):
             piece, block = divmod(index, block_count)
-            held = pieces[piece][:, block * block_size : (block + 1) * block_size]
-            total = total + jnp.where(name == float(target), held.astype(F32), 0.0)
-        source = slice(interior + lanes.start, interior + lanes.stop)
-        for chip in range(rows // row_count):
-            part = slice(chip * row_count, (chip + 1) * row_count)
-            have = gathered[CORES * chip + core, :, source].astype(F32)
-            out[part, lanes] = (have - total[part]).astype(BF16)
+            source = slice(block * block_size, (block + 1) * block_size)
+            here = name == float(target)
+            for row in range(0, rows, tile):
+                held = pieces[piece][row : row + tile, source].astype(F32)
+                have[row // tile] -= jnp.where(here, held, 0.0)
+        out[:, lanes] = jnp.concatenate(have, axis=0).astype(BF16)
 
 
 def interface_kernel(mine, other, inverse, out, reduced):
     core = lax.rem(lax.axis_index("col"), CORES)
-    rows = mine.shape[0]
+    half = mine.shape[0]
 
     @pl.when(core == 0)
     def _():
-        reduced[:rows] = mine[...]
-        reduced[rows:] = other[...]
+        reduced[:half] = mine[...]
+        reduced[half:] = other[...]
 
     @pl.when(core == 1)
     def _():
-        reduced[:rows] = other[...]
-        reduced[rows:] = mine[...]
+        reduced[:half] = other[...]
+        reduced[half:] = mine[...]
 
     out[...] = dot(reduced[...], inverse[...]).astype(BF16)
 
 
-def backward_kernel(block_size, ids, total, gathered, couple, out, picked):
-    slabs, rows, columns = total.shape
-    row_count = gathered.shape[1]
-    own_columns = couple.shape[0]
-    block_count = couple.shape[1] // block_size
+def backward_kernel(block_size, ids, total, own, couple_turned, out, picked):
+    columns = total.shape[2]
+    block_count = couple_turned.shape[0] // block_size
     per_slab = columns // block_size
-    col = lax.axis_index("col")
     for block in range(block_count):
         name = ids[0, block]
         slab = lax.div(name, per_slab)
         offset = pl.multiple_of(lax.rem(name, per_slab) * block_size, block_size)
         picked[:, block * block_size : (block + 1) * block_size] = total[slab, :, pl.ds(offset, block_size)]
-    row = lax.broadcasted_iota(jnp.int32, (rows, rows), 0)
-    place = lax.broadcasted_iota(jnp.int32, (rows, rows), 1)
-    owner = lax.div(row, row_count)
-    held = (
-        lax.rem(owner, CORES) * (rows // CORES)
-        + lax.div(owner, CORES) * row_count
-        + lax.rem(row, row_count)
-    )
-    turn = (held == place).astype(F32).astype(BF16)
-    local = dot(turn, picked[...]).astype(BF16)
-    correction = lax.dot_general(
-        local, couple[...], (((1,), (1,)), ((), ())), preferred_element_type=F32
-    )
-    start = pl.multiple_of(col * own_columns, LANES)
-    for slab in range(slabs):
-        part = slice(slab * row_count, (slab + 1) * row_count)
-        have = gathered[slab, :, pl.ds(start, own_columns)].astype(F32)
-        out[part] = (have - correction[part]).astype(BF16)
+    correction = dot(picked[...], couple_turned[...])
+    out[...] = (own[...].astype(F32) - correction).astype(BF16)
 
 
 def stack_kernel(*refs):
@@ -228,7 +227,7 @@
 def pick_kernel(row_count, total, solution):
     slabs, rows, columns = total.shape
     col = lax.axis_index("col")
-    first = lax.rem(col, CORES) * (rows // CORES) + lax.div(col, CORES) * row_count
+    first = col * row_count
     pick_row = lax.broadcasted_iota(jnp.int32, (8, rows), 0)
     pick_place = lax.broadcasted_iota(jnp.int32, (8, rows), 1)
     pick = (pick_row + first == pick_place).astype(F32).astype(BF16)
@@ -247,7 +246,6 @@
     block_size = local_count // block_count
     col_size = lax.axis_size("col")
     rows = row_count * col_size
-    half = rows // CORES
     width = rhs_interface.shape[1]
     columns = interface_inv.shape[1]
 
@@ -269,8 +267,9 @@
     ids_row = jnp.pad(block_ids, ((0, 0), (0, LANES - block_count)))
 
     core_pairs = [(source, source ^ 1) for source in range(col_size)]
+    half = rows // CORES
     keep, give = run(
-        functools.partial(forward_kernel, half),
+        forward_kernel,
         [(half, local_count)] * 2,
         [gathered, inverse, couple],
         2 * rows * own_columns * (interior + local_count),
@@ -279,17 +278,21 @@
     )
     other = lax.ppermute(give, "col", core_pairs)
     (pair,) = run(add_kernel, [(half, local_count)], [keep, other], half * local_count)
+    plane = exchange(pair, "col", CORES)
+    interface_rows, own_rhs = run(
+        rows_kernel, [(half, width), (rows, own_columns)], [gathered], rows * width
+    )
     (packed,) = run(
         pack_kernel,
         [(half, local_count + LANES)],
-        [pair, *exchange(pair, "col", CORES), ids_row],
+        [pair, *plane, ids_row],
         half * local_count,
     )
     (reduced,) = run(
         functools.partial(place_kernel, block_count, block_size),
         [(half, width)],
-        [gathered, packed, *exchange(packed, "dom")],
-        rows * width * 64,
+        [interface_rows, packed, *exchange(packed, "dom")],
+        half * width * 64,
         limit=16,
     )
     reduced_other = lax.ppermute(reduced, "col", core_pairs)
@@ -300,11 +303,12 @@
         2 * rows * width * columns,
         [pltpu.VMEM((rows, width), BF16)],
     )
+    folds = exchange(part_solution, "dom")
+    (couple_turned,) = run(
+        turn_kernel, [(local_count, own_columns)], [couple], own_columns * local_count
+    )
     (total,) = run(
-        add_kernel,
-        [(rows, columns)],
-        [part_solution, *exchange(part_solution, "dom")],
-        rows * columns,
+        add_kernel, [(rows, columns)], [part_solution, *folds], rows * columns
     )
     every_total = lax.all_gather(total, "col", axis=0)
     interior_rhs = pl.pallas_call(
@@ -320,8 +324,8 @@
     )(
         block_ids,
         pltpu.with_memory_space_constraint(every_total, pltpu.VMEM),
-        pltpu.with_memory_space_constraint(gathered, pltpu.VMEM),
-        pltpu.with_memory_space_constraint(couple, pltpu.VMEM),
+        pltpu.with_memory_space_constraint(own_rhs, pltpu.VMEM),
+        pltpu.with_memory_space_constraint(couple_turned, pltpu.VMEM),
     )
     members = col_size // CORES
     far = exchange(interior_rhs, "col", CORES)

time: 75.1 us -> 74.7 us (level)
    pallas_call x8 -> x10, Pallas kernels: 5.85 us -> 6.4 us  [run(): pl.pallas_call(kernel, out_shape=[jax.ShapeDtypeStruct(shape, BF16) for s...]
  transfers between devices with their start and end apart: 16 -> 16, of which waited for: 12 -> 13; matrix products, arithmetic and copies ran while one was open for 0% -> 0% of each run, Pallas kernels for 4% -> 5%
where the time goes in v4:
time: 74.7 us; the launch traced here: 74.5 us
  blocking collectives  23.6 us (32%)
  waiting for transfers between devices  20.7 us (28%)
  starting transfers between devices  17.1 us (23%)
  Pallas kernels  12.3 us (16%)
  between operations  0.83 us (1%)
    ppermute x12, waiting for transfers between devices, exchange(): pieces.append(lax.ppermute(value, axis, pairs_of(size, shift, stride)))  18.2 us
    ppermute x12, starting transfers between devices, exchange(): pieces.append(lax.ppermute(value, axis, pairs_of(size, shift, stride)))  16 us
    all_gather x1, blocking collectives, per_device(): gathered = lax.all_gather(joined, 'col', axis=0)  13.8 us
    all_gather x1, blocking collectives, per_device(): every_total = lax.all_gather(total, 'col', axis=0)  9.79 us
    pallas_call x10, Pallas kernels, run(): pl.pallas_call(kernel, out_shape=[jax.ShapeDtypeStruct(shape, BF16) for s...  6.4 us
    pallas_call x3, Pallas kernels, product(): pl.pallas_call(kernel, out_shape=jax.ShapeDtypeStruct((rows, inverse.shap...  3.89 us
  transfers between devices with their start and end apart: 16, of which 13 were waited for; matrix products, arithmetic and copies ran while one was open for 0% of the time, Pallas kernels for 5%

profile of v4, /device:TPU:0, one launch (start us, length us, event | category | flops | bytes accessed | tf_op | source)
XLA Modules:
  0.0 74.5 jit_solution(123747291216695698)
XLA Ops:
  0.7 1.1 %shard_map.77 = bf16[6,10240]{1,0:T(8,128)(2,1)S(1)} custom-call(bf16[6,8192]{1,0:T(8,128)(2,1)} %bitcast.18, bf16[6,2048]{1,0:T(8,128)(2,1)} %interface.1), custom_call_target="tpu_custom_call" | custom-call | flops 25769803776 | bytes 1048576 | tf_op jit(solution)/shard_map/pallas_call | solution.py:252
  1.8 13.8 %all-gather.2.gathered = bf16[8,6,10240]{2,1,0:T(8,128)(2,1)S(1)} all-gather(bf16[1,6,10240]{2,1,0:T(8,128)(2,1)S(1)} %bitcast.16), channel_id=2, replica_groups=mesh['dom'=4,'col'=8] {'col'}, dimensions={0}, use_global_device_ids=true | all-gather | bytes 1105920 | tf_op jit(solution)/shard_map/all_gather | solution.py:266
  15.7 3.4 %shard_map.79 = (bf16[24,768]{1,0:T(8,128)(2,1)S(1)}, bf16[24,768]{1,0:T(8,128)(2,1)S(1)}) custom-call(bf16[8,6,10240]{2,1,0:T(8,128)(2,1)S(1)} %all-gather.2.gathered, bf16[8192,1024]{1,0:T(8,128)(2,1)S(1)} %bitcast.8, bf16[1024,768]{1,0:T(8,128)(2,1)S(1)} %bitcast.14), custom_call_target="tpu_custom_call" | custom-call | flops 880803840 | bytes 1048576 | tf_op jit(solution)/shard_map/pallas_call | solution.py:19
  19.5 0.9 %collective-permute-done.refs_1_ = bf16[24,768]{1,0:T(8,128)(2,1)S(1)} collective-permute-done((bf16[24,768]{1,0:T(8,128)(2,1)S(1)}, bf16[24,768]{1,0:T(8,128)(2,1)S(1)}, u32[]{:S(2)}, u32[]{:S(2)}) %collective-permute-start) | collective-permute-done | bytes 36896 | tf_op jit(solution)/shard_map/ppermute | solution.py:279
  20.4 1.0 %collective-permute-start.1 = (bf16[24,768]{1,0:T(8,128)(2,1)S(1)}, bf16[24,768]{1,0:T(8,128)(2,1)S(1)}, u32[]{:S(2)}, u32[]{:S(2)}) collective-permute-start(bf16[24,768]{1,0:T(8,128)(2,1)S(1)} %shard_map.80.refs_0_), channel_id=1, source_target_pairs={{0,2},{1,3},{2,0},{3,1},{4,6},{5,7},{6,4},{7,5},{8,10},{9,11},{10,... | collective-permute-start | bytes 110600 | tf_op jit(solution)/shard_map/ppermute | solution.py:44
  21.4 1.1 %collective-permute-start.2 = (bf16[24,768]{1,0:T(8,128)(2,1)S(1)}, bf16[24,768]{1,0:T(8,128)(2,1)S(1)}, u32[]{:S(2)}, u32[]{:S(2)}) collective-permute-start(bf16[24,768]{1,0:T(8,128)(2,1)S(1)} %shard_map.80.refs_0_), channel_id=1, source_target_pairs={{0,4},{1,5},{2,6},{3,7},{4,0},{5,1},{6,2},{7,3},{8,12},{9,13},{10,... | collective-permute-start | bytes 110600 | tf_op jit(solution)/shard_map/ppermute | solution.py:44
  22.5 1.5 %collective-permute-start.3 = (bf16[24,768]{1,0:T(8,128)(2,1)S(1)}, bf16[24,768]{1,0:T(8,128)(2,1)S(1)}, u32[]{:S(2)}, u32[]{:S(2)}) collective-permute-start(bf16[24,768]{1,0:T(8,128)(2,1)S(1)} %shard_map.80.refs_0_), channel_id=1, source_target_pairs={{0,6},{1,7},{2,4},{3,5},{4,2},{5,3},{6,0},{7,1},{8,14},{9,15},{10,... | collective-permute-start | bytes 110600 | tf_op jit(solution)/shard_map/ppermute | solution.py:44
  24.4 0.9 %collective-permute-done.2.refs_2_ = bf16[24,768]{1,0:T(8,128)(2,1)S(1)} collective-permute-done((bf16[24,768]{1,0:T(8,128)(2,1)S(1)}, bf16[24,768]{1,0:T(8,128)(2,1)S(1)}, u32[]{:S(2)}, u32[]{:S(2)}) %collective-permute-start.2) | collective-permute-done | bytes 36896 | tf_op jit(solution)/shard_map/ppermute | solution.py:44
  25.3 2.0 %collective-permute-done.3.refs_3_ = bf16[24,768]{1,0:T(8,128)(2,1)S(1)} collective-permute-done((bf16[24,768]{1,0:T(8,128)(2,1)S(1)}, bf16[24,768]{1,0:T(8,128)(2,1)S(1)}, u32[]{:S(2)}, u32[]{:S(2)}) %collective-permute-start.3) | collective-permute-done | bytes 36896 | tf_op jit(solution)/shard_map/ppermute | solution.py:44
  27.4 1.6 %collective-permute-start.4 = (bf16[24,896]{1,0:T(8,128)(2,1)S(1)}, bf16[24,896]{1,0:T(8,128)(2,1)S(1)}, u32[]{:S(2)}, u32[]{:S(2)}) collective-permute-start(bf16[24,896]{1,0:T(8,128)(2,1)S(1)} %shard_map.81.refs_0_), channel_id=1, source_target_pairs={{0,8},{8,0},{16,24},{24,16},{1,9},{9,1},{17,25},{25,17},{2,10},{10... | collective-permute-start | bytes 129032 | tf_op jit(solution)/shard_map/ppermute | solution.py:44
  29.0 2.6 %collective-permute-start.5 = (bf16[24,896]{1,0:T(8,128)(2,1)S(1)}, bf16[24,896]{1,0:T(8,128)(2,1)S(1)}, u32[]{:S(2)}, u32[]{:S(2)}) collective-permute-start(bf16[24,896]{1,0:T(8,128)(2,1)S(1)} %shard_map.81.refs_0_), channel_id=1, source_target_pairs={{0,16},{8,24},{16,0},{24,8},{1,17},{9,25},{17,1},{25,9},{2,18},{10... | collective-permute-start | bytes 129032 | tf_op jit(solution)/shard_map/ppermute | solution.py:44
  31.9 3.0 %collective-permute-done.5.refs_2_ = bf16[24,896]{1,0:T(8,128)(2,1)S(1)} collective-permute-done((bf16[24,896]{1,0:T(8,128)(2,1)S(1)}, bf16[24,896]{1,0:T(8,128)(2,1)S(1)}, u32[]{:S(2)}, u32[]{:S(2)}) %collective-permute-start.5) | collective-permute-done | bytes 43040 | tf_op jit(solution)/shard_map/ppermute | solution.py:44
  34.9 2.6 %collective-permute-done.6.refs_3_ = bf16[24,896]{1,0:T(8,128)(2,1)S(1)} collective-permute-done((bf16[24,896]{1,0:T(8,128)(2,1)S(1)}, bf16[24,896]{1,0:T(8,128)(2,1)S(1)}, u32[]{:S(2)}, u32[]{:S(2)}) %collective-permute-start.6) | collective-permute-done | bytes 43040 | tf_op jit(solution)/shard_map/ppermute | solution.py:44
  37.4 0.6 shard_map.82.mine
  38.1 1.3 %collective-permute-done.7.other = bf16[24,2048]{1,0:T(8,128)(2,1)S(1)} collective-permute-done((bf16[24,2048]{1,0:T(8,128)(2,1)S(1)}, bf16[24,2048]{1,0:T(8,128)(2,1)S(1)}, u32[]{:S(2)}, u32[]{:S(2)}) %collective-permute-start.7) | collective-permute-done | bytes 98336 | tf_op jit(solution)/shard_map/ppermute | solution.py:298
  39.4 0.8 %shard_map.83.refs_0_ = bf16[48,1024]{1,0:T(8,128)(2,1)S(1)} custom-call(bf16[24,2048]{1,0:T(8,128)(2,1)S(1)} %shard_map.82.mine, bf16[24,2048]{1,0:T(8,128)(2,1)S(1)} %collective-permute-done.7.other, bf16[2048,1024]{1,0:T(8,128)(2,1)S(1)} %copy-done.1), custom_call_target="tpu_custom_call" | custom-call | flops 201326592 | bytes 1048576 | tf_op jit(solution)/shard_map/pallas_call | solution.py:19
  40.3 0.5 collective-permute-start.10
  40.8 3.9 %collective-permute-start.9 = (bf16[48,1024]{1,0:T(8,128)(2,1)S(1)}, bf16[48,1024]{1,0:T(8,128)(2,1)S(1)}, u32[]{:S(2)}, u32[]{:S(2)}) collective-permute-start(bf16[48,1024]{1,0:T(8,128)(2,1)S(1)} %shard_map.83.refs_0_), channel_id=1, source_target_pairs={{0,16},{8,24},{16,0},{24,8},{1,17},{9,25},{17,1},{25,9},{2,18},{10... | collective-permute-start | bytes 294920 | tf_op jit(solution)/shard_map/ppermute | solution.py:44
  45.2 2.6 %collective-permute-done.10.refs_3_ = bf16[48,1024]{1,0:T(8,128)(2,1)S(1)} collective-permute-done((bf16[48,1024]{1,0:T(8,128)(2,1)S(1)}, bf16[48,1024]{1,0:T(8,128)(2,1)S(1)}, u32[]{:S(2)}, u32[]{:S(2)}) %collective-permute-start.10) | collective-permute-done | bytes 98336 | tf_op jit(solution)/shard_map/ppermute | solution.py:44
  47.9 1.4 %collective-permute-done.8.refs_1_ = bf16[48,1024]{1,0:T(8,128)(2,1)S(1)} collective-permute-done((bf16[48,1024]{1,0:T(8,128)(2,1)S(1)}, bf16[48,1024]{1,0:T(8,128)(2,1)S(1)}, u32[]{:S(2)}, u32[]{:S(2)}) %collective-permute-start.8) | collective-permute-done | bytes 98336 | tf_op jit(solution)/shard_map/ppermute | solution.py:44
  49.2 0.7 collective-permute-done.9.refs_2_
  50.0 9.8 %all-gather.1 = bf16[384,1024]{1,0:T(8,128)(2,1)S(1)} all-gather(bf16[48,1024]{1,0:T(8,128)(2,1)S(1)} %shard_map.84), channel_id=3, replica_groups=mesh['dom'=4,'col'=8] {'col'}, dimensions={0}, use_global_device_ids=true | all-gather | bytes 884736 | tf_op jit(solution)/shard_map/all_gather | solution.py:313
  59.8 0.9 %shard_map.86.refs_0_ = bf16[48,1024]{1,0:T(8,128)(2,1)S(1)} custom-call(s32[1,6]{1,0:T(1,128)S(1)} %copy-done.2, bf16[8,48,1024]{2,1,0:T(8,128)(2,1)S(1)} %bitcast.12, bf16[48,1024]{1,0:T(8,128)(2,1)S(1)} %get-tuple-element.9.own, bf16[768,1024]{1,0:T(8,128)(2,1)S(1)} %shard_map.85.couple_turned), custom_call_target="tpu_custom_call" | custom-call | flops 75497472 | bytes 1048576 | tf_op jit(solution)/shard_map/pallas_call | solution.py:314
  60.7 1.2 %collective-permute-start.12 = (bf16[48,1024]{1,0:T(8,128)(2,1)S(1)}, bf16[48,1024]{1,0:T(8,128)(2,1)S(1)}, u32[]{:S(2)}, u32[]{:S(2)}) collective-permute-start(bf16[48,1024]{1,0:T(8,128)(2,1)S(1)} %shard_map.86.refs_0_), channel_id=1, source_target_pairs={{0,2},{1,3},{2,0},{3,1},{4,6},{5,7},{6,4},{7,5},{8,10},{9,11},{10,... | collective-permute-start | bytes 294920 | tf_op jit(solution)/shard_map/ppermute | solution.py:44
  61.9 0.9 %collective-permute-start.13 = (bf16[48,1024]{1,0:T(8,128)(2,1)S(1)}, bf16[48,1024]{1,0:T(8,128)(2,1)S(1)}, u32[]{:S(2)}, u32[]{:S(2)}) collective-permute-start(bf16[48,1024]{1,0:T(8,128)(2,1)S(1)} %shard_map.86.refs_0_), channel_id=1, source_target_pairs={{0,4},{1,5},{2,6},{3,7},{4,0},{5,1},{6,2},{7,3},{8,12},{9,13},{10,... | collective-permute-start | bytes 294920 | tf_op jit(solution)/shard_map/ppermute | solution.py:44
  62.8 1.5 %collective-permute-start.14 = (bf16[48,1024]{1,0:T(8,128)(2,1)S(1)}, bf16[48,1024]{1,0:T(8,128)(2,1)S(1)}, u32[]{:S(2)}, u32[]{:S(2)}) collective-permute-start(bf16[48,1024]{1,0:T(8,128)(2,1)S(1)} %shard_map.86.refs_0_), channel_id=1, source_target_pairs={{0,6},{1,7},{2,4},{3,5},{4,2},{5,3},{6,0},{7,1},{8,14},{9,15},{10,... | collective-permute-start | bytes 294920 | tf_op jit(solution)/shard_map/ppermute | solution.py:44
  64.3 1.6 %collective-permute-done.12.refs_0_ = bf16[48,1024]{1,0:T(8,128)(2,1)S(1)} collective-permute-done((bf16[48,1024]{1,0:T(8,128)(2,1)S(1)}, bf16[48,1024]{1,0:T(8,128)(2,1)S(1)}, u32[]{:S(2)}, u32[]{:S(2)}) %collective-permute-start.12) | collective-permute-done | bytes 98336 | tf_op jit(solution)/shard_map/ppermute | solution.py:44
  65.9 2.9 %collective-permute-done.13.refs_1_ = bf16[48,1024]{1,0:T(8,128)(2,1)S(1)} collective-permute-done((bf16[48,1024]{1,0:T(8,128)(2,1)S(1)}, bf16[48,1024]{1,0:T(8,128)(2,1)S(1)}, u32[]{:S(2)}, u32[]{:S(2)}) %collective-permute-start.13) | collective-permute-done | bytes 98336 | tf_op jit(solution)/shard_map/ppermute | solution.py:44
  69.4 0.9 %shard_map.91 = bf16[6,8192]{1,0:T(8,128)(2,1)} custom-call(bf16[8,48,1024]{2,1,0:T(8,128)(2,1)S(1)} %bitcast.13), custom_call_target="tpu_custom_call" | custom-call | flops 6291456 | bytes 1048576 | tf_op jit(solution)/shard_map/pallas_call | solution.py:19
  70.6 0.8 %shard_map.87.carry = f32[48,1024]{1,0:T(8,128)S(1)} custom-call(bf16[8192,1024]{1,0:T(8,128)(2,1)S(1)} %bitcast.9, bf16[48,1024]{1,0:T(8,128)(2,1)S(1)} %shard_map.86.refs_0_, bf16[48,1024]{1,0:T(8,128)(2,1)S(1)} %collective-permute-done.11.refs_1_), custom_call_target="tpu_custom_call" | custom-call | flops 201326592 | bytes 1048576 | tf_op jit(solution)/shard_map/pallas_call | solution.py:213
  71.5 1.2 %shard_map.89.carry = f32[48,1024]{1,0:T(8,128)S(1)} custom-call(bf16[8192,1024]{1,0:T(8,128)(2,1)S(1)} %bitcast.10, f32[48,1024]{1,0:T(8,128)S(1)} %shard_map.87.carry, bf16[3,48,1024]{2,1,0:T(8,128)(2,1)S(1)} %shard_map.88.refs_0_), custom_call_target="tpu_custom_call" | custom-call | flops 301989888 | bytes 1048576 | tf_op jit(solution)/shard_map/pallas_call | solution.py:213
  72.7 1.9 %shard_map.90 = bf16[48,1024]{1,0:T(8,128)(2,1)} custom-call(bf16[8192,1024]{1,0:T(8,128)(2,1)S(1)} %bitcast.11, f32[48,1024]{1,0:T(8,128)S(1)} %shard_map.89.carry, bf16[3,48,1024]{2,1,0:T(8,128)(2,1)S(1)} %collective-permute-done.15.refs_0_), custom_call_target="tpu_custom_call" | custom-call | flops 301989888 | bytes 1048576 | tf_op jit(solution)/shard_map/pallas_call | solution.py:213
  (33 shorter events, 2.8 us)
Async XLA Ops:
  0.6 15.0 %slice-start = ((s8[16777216]{0:T(1024)(128)(4,1)}), s8[4194304]{0:T(1024)(128)(4,1)S(1)}, s32[]{:S(2)}) async-start(s8[16777216]{0:T(1024)(128)(4,1)} %bitcast.6), calls=%async_computation | async-start | bytes 8388608
  0.6 15.0 %slice-start.1 = ((s8[16777216]{0:T(1024)(128)(4,1)}), s8[4194304]{0:T(1024)(128)(4,1)S(1)}, s32[]{:S(2)}) async-start(s8[16777216]{0:T(1024)(128)(4,1)} %bitcast.6), calls=%async_computation.1 | async-start | bytes 8388608
  0.7 15.0 %slice-start.2 = ((s8[16777216]{0:T(1024)(128)(4,1)}), s8[4194304]{0:T(1024)(128)(4,1)S(1)}, s32[]{:S(2)}) async-start(s8[16777216]{0:T(1024)(128)(4,1)} %bitcast.6), calls=%async_computation.2 | async-start | bytes 8388608
  0.7 14.9 %slice-start.3 = ((s8[16777216]{0:T(1024)(128)(4,1)}), s8[4194304]{0:T(1024)(128)(4,1)S(1)}, s32[]{:S(2)}) async-start(s8[16777216]{0:T(1024)(128)(4,1)} %bitcast.6), calls=%async_computation.3 | async-start | bytes 8388608
  0.7 14.9 %copy-start = (bf16[1,1024,768]{2,1,0:T(8,128)(2,1)S(1)}, bf16[1,1024,768]{2,1,0:T(8,128)(2,1)}, u32[]{:S(2)}) copy-start(bf16[1,1024,768]{2,1,0:T(8,128)(2,1)} %param.8) | copy-start | bytes 4718596
  15.6 8.3 %copy-start.2 = (s32[1,6]{1,0:T(1,128)S(1)}, s32[1,6]{1,0:T(1,128)}, u32[]{:S(2)}) copy-start(s32[1,6]{1,0:T(1,128)} %ids.1) | copy-start | bytes 76
  15.6 23.8 %copy-start.1 = (bf16[2048,1024]{1,0:T(8,128)(2,1)S(1)}, bf16[2048,1024]{1,0:T(8,128)(2,1)}, u32[]{:S(2)}) copy-start(bf16[2048,1024]{1,0:T(8,128)(2,1)} %inverse.1) | copy-start | bytes 12582916
  19.1 1.3 %collective-permute-start = (bf16[24,768]{1,0:T(8,128)(2,1)S(1)}, bf16[24,768]{1,0:T(8,128)(2,1)S(1)}, u32[]{:S(2)}, u32[]{:S(2)}) collective-permute-start(bf16[24,768]{1,0:T(8,128)(2,1)S(1)} %get-tuple-element.8), channel_id=1, source_target_pairs={{0,1},{1,0},{2,3},{3,2},{4,5},{5,4},{6,7},{7,6},{8,9},{9,8},{10,11... | collective-permute-start | bytes 110600 | tf_op jit(solution)/shard_map/ppermute | solution.py:279
  20.4 4.0 %collective-permute-start.1 = (bf16[24,768]{1,0:T(8,128)(2,1)S(1)}, bf16[24,768]{1,0:T(8,128)(2,1)S(1)}, u32[]{:S(2)}, u32[]{:S(2)}) collective-permute-start(bf16[24,768]{1,0:T(8,128)(2,1)S(1)} %shard_map.80.refs_0_), channel_id=1, source_target_pairs={{0,2},{1,3},{2,0},{3,1},{4,6},{5,7},{6,4},{7,5},{8,10},{9,11},{10,... | collective-permute-start | bytes 110600 | tf_op jit(solution)/shard_map/ppermute | solution.py:44
  21.4 4.0 %collective-permute-start.2 = (bf16[24,768]{1,0:T(8,128)(2,1)S(1)}, bf16[24,768]{1,0:T(8,128)(2,1)S(1)}, u32[]{:S(2)}, u32[]{:S(2)}) collective-permute-start(bf16[24,768]{1,0:T(8,128)(2,1)S(1)} %shard_map.80.refs_0_), channel_id=1, source_target_pairs={{0,4},{1,5},{2,6},{3,7},{4,0},{5,1},{6,2},{7,3},{8,12},{9,13},{10,... | collective-permute-start | bytes 110600 | tf_op jit(solution)/shard_map/ppermute | solution.py:44
  22.5 4.9 %collective-permute-start.3 = (bf16[24,768]{1,0:T(8,128)(2,1)S(1)}, bf16[24,768]{1,0:T(8,128)(2,1)S(1)}, u32[]{:S(2)}, u32[]{:S(2)}) collective-permute-start(bf16[24,768]{1,0:T(8,128)(2,1)S(1)} %shard_map.80.refs_0_), channel_id=1, source_target_pairs={{0,6},{1,7},{2,4},{3,5},{4,2},{5,3},{6,0},{7,1},{8,14},{9,15},{10,... | collective-permute-start | bytes 110600 | tf_op jit(solution)/shard_map/ppermute | solution.py:44
  27.4 4.5 %collective-permute-start.4 = (bf16[24,896]{1,0:T(8,128)(2,1)S(1)}, bf16[24,896]{1,0:T(8,128)(2,1)S(1)}, u32[]{:S(2)}, u32[]{:S(2)}) collective-permute-start(bf16[24,896]{1,0:T(8,128)(2,1)S(1)} %shard_map.81.refs_0_), channel_id=1, source_target_pairs={{0,8},{8,0},{16,24},{24,16},{1,9},{9,1},{17,25},{25,17},{2,10},{10... | collective-permute-start | bytes 129032 | tf_op jit(solution)/shard_map/ppermute | solution.py:44
  29.0 5.8 %collective-permute-start.5 = (bf16[24,896]{1,0:T(8,128)(2,1)S(1)}, bf16[24,896]{1,0:T(8,128)(2,1)S(1)}, u32[]{:S(2)}, u32[]{:S(2)}) collective-permute-start(bf16[24,896]{1,0:T(8,128)(2,1)S(1)} %shard_map.81.refs_0_), channel_id=1, source_target_pairs={{0,16},{8,24},{16,0},{24,8},{1,17},{9,25},{17,1},{25,9},{2,18},{10... | collective-permute-start | bytes 129032 | tf_op jit(solution)/shard_map/ppermute | solution.py:44
  31.6 5.8 %collective-permute-start.6 = (bf16[24,896]{1,0:T(8,128)(2,1)S(1)}, bf16[24,896]{1,0:T(8,128)(2,1)S(1)}, u32[]{:S(2)}, u32[]{:S(2)}) collective-permute-start(bf16[24,896]{1,0:T(8,128)(2,1)S(1)} %shard_map.81.refs_0_), channel_id=1, source_target_pairs={{0,24},{8,16},{16,8},{24,0},{1,25},{9,17},{17,9},{25,1},{2,26},{10... | collective-permute-start | bytes 129032 | tf_op jit(solution)/shard_map/ppermute | solution.py:44
  38.0 1.4 %collective-permute-start.7 = (bf16[24,2048]{1,0:T(8,128)(2,1)S(1)}, bf16[24,2048]{1,0:T(8,128)(2,1)S(1)}, u32[]{:S(2)}, u32[]{:S(2)}) collective-permute-start(bf16[24,2048]{1,0:T(8,128)(2,1)S(1)} %shard_map.82.mine), channel_id=1, source_target_pairs={{0,1},{1,0},{2,3},{3,2},{4,5},{5,4},{6,7},{7,6},{8,9},{9,8},{10,11... | collective-permute-start | bytes 294920 | tf_op jit(solution)/shard_map/ppermute | solution.py:298
  40.3 7.6 %collective-permute-start.10 = (bf16[48,1024]{1,0:T(8,128)(2,1)S(1)}, bf16[48,1024]{1,0:T(8,128)(2,1)S(1)}, u32[]{:S(2)}, u32[]{:S(2)}) collective-permute-start(bf16[48,1024]{1,0:T(8,128)(2,1)S(1)} %shard_map.83.refs_0_), channel_id=1, source_target_pairs={{0,24},{8,16},{16,8},{24,0},{1,25},{9,17},{17,9},{25,1},{2,26},{10... | collective-permute-start | bytes 294920 | tf_op jit(solution)/shard_map/ppermute | solution.py:44
  40.8 8.5 %collective-permute-start.8 = (bf16[48,1024]{1,0:T(8,128)(2,1)S(1)}, bf16[48,1024]{1,0:T(8,128)(2,1)S(1)}, u32[]{:S(2)}, u32[]{:S(2)}) collective-permute-start(bf16[48,1024]{1,0:T(8,128)(2,1)S(1)} %shard_map.83.refs_0_), channel_id=1, source_target_pairs={{0,8},{8,0},{16,24},{24,16},{1,9},{9,1},{17,25},{25,17},{2,10},{10... | collective-permute-start | bytes 294920 | tf_op jit(solution)/shard_map/ppermute | solution.py:44
  40.8 9.2 %collective-permute-start.9 = (bf16[48,1024]{1,0:T(8,128)(2,1)S(1)}, bf16[48,1024]{1,0:T(8,128)(2,1)S(1)}, u32[]{:S(2)}, u32[]{:S(2)}) collective-permute-start(bf16[48,1024]{1,0:T(8,128)(2,1)S(1)} %shard_map.83.refs_0_), channel_id=1, source_target_pairs={{0,16},{8,24},{16,0},{24,8},{1,17},{9,25},{17,1},{25,9},{2,18},{10... | collective-permute-start | bytes 294920 | tf_op jit(solution)/shard_map/ppermute | solution.py:44
  60.7 5.2 %collective-permute-start.12 = (bf16[48,1024]{1,0:T(8,128)(2,1)S(1)}, bf16[48,1024]{1,0:T(8,128)(2,1)S(1)}, u32[]{:S(2)}, u32[]{:S(2)}) collective-permute-start(bf16[48,1024]{1,0:T(8,128)(2,1)S(1)} %shard_map.86.refs_0_), channel_id=1, source_target_pairs={{0,2},{1,3},{2,0},{3,1},{4,6},{5,7},{6,4},{7,5},{8,10},{9,11},{10,... | collective-permute-start | bytes 294920 | tf_op jit(solution)/shard_map/ppermute | solution.py:44
  61.9 6.9 %collective-permute-start.13 = (bf16[48,1024]{1,0:T(8,128)(2,1)S(1)}, bf16[48,1024]{1,0:T(8,128)(2,1)S(1)}, u32[]{:S(2)}, u32[]{:S(2)}) collective-permute-start(bf16[48,1024]{1,0:T(8,128)(2,1)S(1)} %shard_map.86.refs_0_), channel_id=1, source_target_pairs={{0,4},{1,5},{2,6},{3,7},{4,0},{5,1},{6,2},{7,3},{8,12},{9,13},{10,... | collective-permute-start | bytes 294920 | tf_op jit(solution)/shard_map/ppermute | solution.py:44
  62.8 6.0 %collective-permute-start.14 = (bf16[48,1024]{1,0:T(8,128)(2,1)S(1)}, bf16[48,1024]{1,0:T(8,128)(2,1)S(1)}, u32[]{:S(2)}, u32[]{:S(2)}) collective-permute-start(bf16[48,1024]{1,0:T(8,128)(2,1)S(1)} %shard_map.86.refs_0_), channel_id=1, source_target_pairs={{0,6},{1,7},{2,4},{3,5},{4,2},{5,3},{6,0},{7,1},{8,14},{9,15},{10,... | collective-permute-start | bytes 294920 | tf_op jit(solution)/shard_map/ppermute | solution.py:44
  68.8 3.8 %collective-permute-start.15 = (bf16[3,48,1024]{2,1,0:T(8,128)(2,1)S(1)}, bf16[3,48,1024]{2,1,0:T(8,128)(2,1)S(1)}, u32[]{:S(2)}, u32[]{:S(2)}) collective-permute-start(bf16[3,48,1024]{2,1,0:T(8,128)(2,1)S(1)} %shard_map.88.refs_0_), channel_id=1, source_target_pairs={{0,1},{1,0},{2,3},{3,2},{4,5},{5,4},{6,7},{7,6},{8,9},{9,8},{10,11... | collective-permute-start | bytes 884744 | tf_op jit(solution)/shard_map/ppermute | solution.py:342
  68.9 1.7 %collective-permute-start.11 = (bf16[48,1024]{1,0:T(8,128)(2,1)S(1)}, bf16[48,1024]{1,0:T(8,128)(2,1)S(1)}, u32[]{:S(2)}, u32[]{:S(2)}) collective-permute-start(bf16[48,1024]{1,0:T(8,128)(2,1)S(1)} %shard_map.86.refs_0_), channel_id=1, source_target_pairs={{0,1},{1,0},{2,3},{3,2},{4,5},{5,4},{6,7},{7,6},{8,9},{9,8},{10,11... | collective-permute-start | bytes 294920 | tf_op jit(solution)/shard_map/ppermute | solution.py:332
